TPU v7x, 512 devices: a whole 4x8x8 slice. The times are simulated.
512 devices in a mesh: hi: 4 (over z_hi, core), mid: 4 (over x), lo: 32 (over z_lo, y).
Axes of the slice: x: 4, y: 8, z: 8 (z_hi: 2, z_lo: 4; z = z_hi * 4 + z_lo), core: 2. Of those that a mesh axis runs over, the one named last changes fastest.
Arguments:
- amplitudes: bfloat16 [16384, 16384], P('lo', ('hi', 'mid')), may hold values from -6 to 6
- hop_blocks: bfloat16 [4, 512, 512], replicated, may hold values from -1 to 2, as said below
- coupling_seed: int32 [14], replicated, may hold values from 1 to 7
Outputs:
- new_state: bfloat16 [16384, 16384], P('lo', ('hi', 'mid'))
Inputs may be any that keep to these rules, and one draw needn't show every extreme that they name: hop_blocks[k, a, b] is zero where a and b differ in their number of set bits.
All inputs are finite; a program needn't handle non-finite values.
Results may differ from a plain program's by a relative error of at most 0.0064.
Values may be sent and summed in bfloat16 or wider, within the bound.
No kernel may reach another device: no remote copies, remote signals or barrier semaphores. Data moves between devices by JAX's collectives and lax.ppermute only.
A program may use at most 64 MiB of HBM per device.

v0:
```python
import jax
import jax.numpy as jnp
from jax import lax
from jax.sharding import PartitionSpec as P

BLOCK = 512
SITES = 14


COUPLING = 0.06


def occupancy(indices):
    site_ids = jnp.arange(SITES, dtype=jnp.int32)
    return (indices[:, None] >> site_ids[None, :] & 1).astype(jnp.float32)


def diagonal_factor(up_index, down_index, coupling_seed):
    up_occupied = occupancy(up_index)
    down_occupied = occupancy(down_index)
    strength = COUPLING * coupling_seed.astype(jnp.float32)
    energy = jnp.dot(
        up_occupied * strength[None, :], down_occupied.T, precision=lax.Precision.HIGHEST
    )
    return jnp.exp(-energy)


def on_device(amplitudes, hop_blocks, coupling_seed):
    down_rows, up_cols = amplitudes.shape
    groups = lax.axis_size(("hi", "mid"))
    lo_count = lax.axis_size("lo")
    split_view = amplitudes.reshape(down_rows, up_cols // BLOCK, BLOCK)
    first_pass = jnp.einsum(
        "dav,wv->awd", split_view, hop_blocks[0], preferred_element_type=jnp.float32
    ).astype(jnp.bfloat16)
    local_top = BLOCK // groups
    remainder = up_cols // local_top
    first_pass = first_pass.reshape(local_top, remainder, down_rows)
    moved = lax.all_to_all(first_pass, ("hi", "mid"), split_axis=1, concat_axis=0, tiled=True)
    second_pass = jnp.einsum(
        "gh,hpd->gpd", hop_blocks[1], moved, preferred_element_type=jnp.float32
    )
    span_low = remainder // groups
    up_index = (
        jnp.arange(BLOCK, dtype=jnp.int32)[:, None] * remainder
        + lax.axis_index(("hi", "mid")) * span_low
        + jnp.arange(span_low, dtype=jnp.int32)[None, :]
    ).reshape(-1)
    down_index = lax.axis_index("lo") * down_rows + jnp.arange(down_rows, dtype=jnp.int32)
    factor = diagonal_factor(up_index, down_index, coupling_seed).reshape(
        BLOCK, span_low, down_rows
    )
    mixed_pass = (second_pass * factor).astype(jnp.bfloat16)
    returned = lax.all_to_all(
        mixed_pass, ("hi", "mid"), split_axis=0, concat_axis=1, tiled=True
    ).reshape(up_cols, down_rows)
    third_pass = jnp.einsum(
        "ud,ed->eu", returned, hop_blocks[2], preferred_element_type=jnp.float32
    ).astype(jnp.bfloat16)
    gathered = lax.all_to_all(
        third_pass.reshape(BLOCK // lo_count, lo_count, up_cols),
        "lo",
        split_axis=1,
        concat_axis=0,
        tiled=True,
    )
    fourth_pass = jnp.einsum(
        "gh,hpu->gpu", hop_blocks[3], gathered, preferred_element_type=jnp.float32
    ).astype(jnp.bfloat16)
    result = lax.all_to_all(fourth_pass, "lo", split_axis=0, concat_axis=1, tiled=True).reshape(
        down_rows, up_cols
    )
    return result


def solution(mesh):
    in_specs = (P("lo", ("hi", "mid")), P(), P())
    out_specs = P("lo", ("hi", "mid"))
    return jax.shard_map(
        on_device, mesh=mesh, in_specs=in_specs, out_specs=out_specs, check_vma=False
    )
```

profile of v0, /device:TPU:4, one launch (start us, length us, event | category | flops | bytes accessed | tf_op | source)
XLA Modules:
  0.0 168.0 jit_solution(16934776479750978386)
XLA Ops:
  0.0 2.1 %convolution_convert_fusion.2 = bf16[512,512,2]{1,0,2:T(8,128)(2,1)S(1)} fusion(bf16[64,2,8,512]{3,2,1,0:T(8,128)(2,1)} %bitcast.58, bf16[4,512,512]{2,1,0:T(8,128)(2,1)} %param.4), kind=kOutput, calls=%fused_computation.5 | convolution fusion | flops 537395200 | bytes 2621440 | tf_op jit(solution)/shard_map/dav,wv->awd/dot_general | solution.py:33
  2.1 0.0 copy-start
  2.1 1.5 copy.36
  3.7 13.3 %all-to-all-start = ((bf16[32,32,512]{2,0,1:T(8,128)(2,1)}), bf16[32,32,512]{2,0,1:T(8,128)(2,1)S(1)}, u32[]{:S(2)}, u32[]{:S(2)}) async-start(bf16[32,32,512]{2,0,1:T(8,128)(2,1)} %copy.36), calls=%async_computation | async-start | bytes 2097152 | tf_op jit(solution)/shard_map/all_to_all | solution.py:39
  17.0 0.1 iota_add_fusion
  17.1 0.2 add.50
  17.3 0.0 copy-done
  17.3 2.0 %negate_exponential_fusion = f32[1024,512]{1,0:T(8,128)S(1)} fusion(s32[512]{0:T(512)S(1)} %iota_add_fusion.1, f32[14]{0:T(128)S(1)} %convert_multiply_fusion, s32[1024]{0:T(1024)S(1)} %add.50), kind=kOutput, calls=%fused_computation.2 | convolution fusion | flops 88683520 | bytes 2103352 | tf_op jit(solution)/shard_map/dot_general | solution.py:22
  19.3 2.3 %reshape.54 = f32[512,2,512]{2,1,0:T(2,128)} reshape(f32[1024,512]{1,0:T(8,128)S(1)} %negate_exponential_fusion) | data formatting | bytes 4194304 | tf_op jit(solution)/shard_map/reshape | solution.py:50
  21.6 2.7 %copy.39 = f32[512,2,512]{0,2,1:T(8,128)S(1)} copy(f32[512,2,512]{2,1,0:T(2,128)} %reshape.54) | data formatting | bytes 4194304 | tf_op jit(solution)/shard_map/reshape | solution.py:50
  24.4 8.8 %all-to-all-done = bf16[32,32,512]{2,0,1:T(8,128)(2,1)S(1)} async-done(((bf16[32,32,512]{2,0,1:T(8,128)(2,1)}), bf16[32,32,512]{2,0,1:T(8,128)(2,1)S(1)}, u32[]{:S(2)}, u32[]{:S(2)}) %all-to-all-start) | async-done | bytes 1048608 | tf_op jit(solution)/shard_map/all_to_all | solution.py:39
  33.2 0.1 copy.37
  33.3 1.8 %fusion = bf16[512,2,512]{0,2,1:T(8,128)(2,1)S(1)} fusion(f32[512,2,512]{0,2,1:T(8,128)S(1)} %copy.39, bf16[512,2,512]{2,0,1:T(8,128)(2,1)S(1)} %bitcast.54, bf16[4,512,512]{2,1,0:T(8,128)(2,1)} %param.4), kind=kOutput, calls=%fused_computation.1 | convolution fusion | flops 537919488 | bytes 4718592 | tf_op jit(solution)/shard_map/gh,hpd->gpd/dot_general | solution.py:40
  35.1 1.0 copy.40
  36.1 34.2 %all_to_all.63 = bf16[512,2,512]{2,1,0:T(2,128)(2,1)S(1)} all-to-all(bf16[512,2,512]{2,1,0:T(2,128)(2,1)S(1)} %copy.40), channel_id=1, replica_groups=mesh['hi'=4,'mid'=4,'lo'=32] {'hi','mid'}, dimensions={0} | all-to-all | bytes 2097152 | tf_op jit(solution)/shard_map/all_to_all | solution.py:54
  70.3 0.2 copy.41
  70.5 1.1 copy.42
  71.6 0.4 reshape.55
  72.0 1.8 %convolution_convert_fusion.1 = bf16[1024,512]{0,1:T(8,128)(2,1)S(1)} fusion(bf16[1024,512]{1,0:T(8,128)(2,1)S(1)} %reshape.55, bf16[4,512,512]{2,1,0:T(8,128)(2,1)} %param.4), kind=kOutput, calls=%fused_computation.4 | convolution fusion | flops 537395200 | bytes 2621440 | tf_op jit(solution)/shard_map/ud,ed->eu/dot_general | solution.py:57
  73.8 0.6 copy.43
  74.4 51.7 %all_to_all.64 = bf16[16,32,1024]{2,0,1:T(8,128)(2,1)S(1)} all-to-all(bf16[16,32,1024]{2,0,1:T(8,128)(2,1)S(1)} %copy.43), channel_id=1, replica_groups=mesh['hi'=4,'mid'=4,'lo'=32] {'lo'}, dimensions={1} | all-to-all | bytes 2097152 | tf_op jit(solution)/shard_map/all_to_all | solution.py:60
  126.1 1.8 %fusion.1 = bf16[512,1,1024]{0,2,1:T(8,128)(2,1)S(1)} fusion(bf16[512,1024]{1,0:T(8,128)(2,1)S(1)} %bitcast.56, bf16[4,512,512]{2,1,0:T(8,128)(2,1)} %param.4), kind=kOutput, calls=%fused_computation.6 | convolution fusion | flops 537395200 | bytes 2621440 | tf_op jit(solution)/shard_map/gh,hpu->gpu/dot_general | solution.py:67
  127.9 0.5 broadcast.24
  128.4 1.5 reduce
  129.9 0.5 copy.53
  130.4 0.8 reshape.61
  131.2 33.8 %all_to_all.65 = bf16[32,2,8192]{2,1,0:T(2,128)(2,1)S(1)} all-to-all(bf16[32,2,8192]{2,1,0:T(2,128)(2,1)S(1)} %reshape.61), channel_id=1, replica_groups=mesh['hi'=4,'mid'=4,'lo'=32] {'lo'}, dimensions={0} | all-to-all | bytes 2097152 | tf_op jit(solution)/shard_map/all_to_all | solution.py:70
  165.0 1.0 reshape.62
  166.0 0.4 copy.47
  166.4 1.5 copy.45
  (3 shorter events, 0.0 us)
Async XLA Ops:
  2.1 15.2 %copy-start = (s32[14]{0:T(128)S(1)}, s32[14]{0:T(128)}, u32[]{:S(2)}) copy-start(s32[14]{0:T(128)} %param.5) | copy-start | bytes 172
  3.7 29.5 %all-to-all-start = ((bf16[32,32,512]{2,0,1:T(8,128)(2,1)}), bf16[32,32,512]{2,0,1:T(8,128)(2,1)S(1)}, u32[]{:S(2)}, u32[]{:S(2)}) async-start(bf16[32,32,512]{2,0,1:T(8,128)(2,1)} %copy.36), calls=%async_computation | async-start | bytes 2097152 | tf_op jit(solution)/shard_map/all_to_all | solution.py:39
where the time goes:
time: 168 us
  blocking collectives  120 us (71%)
  local copies, waits for them, and re-layouts  14.9 us (9%)
  starting transfers between devices  13.3 us (8%)
  matrix products  9.52 us (6%)
  waiting for transfers between devices  8.83 us (5%)
    all_to_all x1, blocking collectives, on_device(): lax.all_to_all(third_pass.reshape(BLOCK // lo_count, lo_count, up_cols),...  51.7 us
    all_to_all x1, blocking collectives, on_device(): lax.all_to_all(mixed_pass, ('hi', 'mid'), split_axis=0, concat_axis=1, ti...  34.2 us
    all_to_all x1, blocking collectives, on_device(): lax.all_to_all(fourth_pass, 'lo', split_axis=0, concat_axis=1, tiled=True)  33.8 us
    all_to_all x1, starting transfers between devices, on_device(): lax.all_to_all(first_pass, ('hi', 'mid'), split_axis=1, concat_axis=0, ti...  13.3 us
    all_to_all x1, waiting for transfers between devices, on_device(): lax.all_to_all(first_pass, ('hi', 'mid'), split_axis=1, concat_axis=0, ti...  8.83 us
    reshape x2, local copies, waits for them, and re-layouts, on_device(): diagonal_factor(up_index, down_index, coupling_seed)  5.05 us
  transfers between devices with their start and end apart: 1, of which 1 were waited for; matrix products, arithmetic and copies ran while one was open for 4% of the time, Pallas kernels for 0%

commit v1 on v0

v1 whole, which is shorter than its diff:
```python
import jax
import jax.numpy as jnp
from jax import lax
from jax.sharding import Mesh, PartitionSpec as P

BLOCK = 512
SITES = 14
COUPLING = 0.06

AXES = ("zh", "core", "x", "z1", "z0", "yh", "y0")
SIZES = (2, 2, 4, 2, 2, 4, 2)
EX1 = ("zh", "core", "x", "z1", "yh")
EX2 = ("x", "z0", "y0")
EX3 = ("yh", "y0", "zh", "z1", "z0", "core")


def exchange(value, axes):
    return lax.all_to_all(value, axes, split_axis=0, concat_axis=0, tiled=True)


def bits(index, width):
    return [(index >> (width - 1 - b)) & 1 for b in range(width)]


def interaction(coupling_seed):
    c = COUPLING * coupling_seed.astype(jnp.float32)
    zh, core, x = lax.axis_index("zh"), lax.axis_index("core"), lax.axis_index("x")
    z1, z0 = lax.axis_index("z1"), lax.axis_index("z0")
    yh, y0 = lax.axis_index("yh"), lax.axis_index("y0")
    g = jnp.arange(8, dtype=jnp.int32)
    lane = jnp.arange(128, dtype=jnp.int32)
    k = jnp.arange(BLOCK, dtype=jnp.int32)
    u_low = (zh << 4) | (core << 3) | (z1 << 2) | yh
    u = (k << 5) | u_low
    d = (
        ((g[:, None] >> 2) << 13)
        | (z0 << 12)
        | ((g[:, None] & 3) << 10)
        | (y0 << 9)
        | (x << 7)
        | lane[None, :]
    )
    sites = jnp.arange(SITES, dtype=jnp.int32)
    nu = ((u[:, None] >> sites) & 1).astype(jnp.float32)
    nd = ((d.reshape(-1)[:, None] >> sites) & 1).astype(jnp.float32)
    energy = jnp.dot(nu * c, nd.T, precision=lax.Precision.HIGHEST)
    return jnp.exp(-energy).reshape(BLOCK, 8, 128).transpose(1, 0, 2)


def step_one(amplitudes, hop):
    first = jnp.einsum(
        "dav,wv->awd", amplitudes.reshape(512, 2, 512), hop, preferred_element_type=jnp.float32
    ).astype(jnp.bfloat16)
    first = first.reshape(2, 16, 4, 2, 4, 4, 128).transpose(2, 5, 3, 4, 0, 1, 6)
    return first.reshape(128, 32, 128)


def step_two(moved, hop, factor):
    moved = moved.reshape(16, 8, 32, 128).transpose(1, 0, 2, 3).reshape(8, 512, 128)
    second = jnp.einsum("kj,gjl->gkl", hop, moved, preferred_element_type=jnp.float32)
    mixed = (second * factor).astype(jnp.bfloat16)
    mixed = mixed.reshape(8, 4, 16, 2, 4, 128).transpose(2, 0, 4, 1, 3, 5)
    return mixed.reshape(16, 8 * 4 * 8, 128)


def step_three_four(moved, hop_low, hop_high):
    data = moved.reshape(4, 1024, 128).transpose(1, 0, 2).reshape(1024, 512)
    third = jnp.einsum("nd,ed->ne", data, hop_low, preferred_element_type=jnp.float32)
    third = third.astype(jnp.bfloat16)
    third = third.reshape(2, 2, 2, 4, 4, 4, 2, 16, 32).transpose(2, 0, 3, 1, 7, 5, 6, 4, 8)
    third = third.reshape(512, 1024)
    fourth = jnp.einsum("gh,hn->gn", hop_high, third, preferred_element_type=jnp.float32)
    fourth = fourth.astype(jnp.bfloat16)
    fourth = fourth.reshape(2, 2, 4, 2, 16, 2, 2, 2, 4, 32).transpose(2, 3, 5, 0, 1, 6, 7, 4, 8, 9)
    return fourth.reshape(128, 32, 128)


def finish(moved):
    moved = moved.reshape(4, 2, 2, 2, 2, 2, 2, 16, 4, 32)
    return moved.transpose(7, 9, 4, 1, 6, 8, 2, 5, 3, 0).reshape(512, 1024)


def on_device(amplitudes, hop_blocks, coupling_seed):
    sent = exchange(step_one(amplitudes, hop_blocks[0]), EX1)
    factor = interaction(coupling_seed)
    sent = exchange(step_two(sent, hop_blocks[1], factor), EX2)
    sent = exchange(step_three_four(sent, hop_blocks[2], hop_blocks[3]), EX3)
    return finish(sent)


def solution(mesh):
    fine = Mesh(mesh.devices.reshape(SIZES), AXES)
    spec = P(("z1", "z0", "yh", "y0"), ("zh", "core", "x"))
    return jax.shard_map(
        on_device, mesh=fine, in_specs=(spec, P(), P()), out_specs=spec, check_vma=False
    )
```

time: 168 us -> 178 us (1.060)
  the two profiles are of different devices: /device:TPU:4 before, /device:TPU:1 now
where the time goes in v1:
time: 178 us; the launch traced here: 177 us
  local copies, waits for them, and re-layouts  59.1 us (33%)
  blocking collectives  56.5 us (32%)
  waiting for transfers between devices  29.6 us (17%)
  starting transfers between devices  21 us (12%)
  matrix products  11 us (6%)
    all_to_all x2, blocking collectives, exchange(): return lax.all_to_all(value, axes, split_axis=0, concat_axis=0, tiled=True)  56.5 us
    all_to_all x1, waiting for transfers between devices, exchange(): return lax.all_to_all(value, axes, split_axis=0, concat_axis=0, tiled=True)  29.6 us
    all_to_all x1, starting transfers between devices, exchange(): return lax.all_to_all(value, axes, split_axis=0, concat_axis=0, tiled=True)  21 us
    reshape x2, local copies, waits for them, and re-layouts, step_three_four(): third.reshape(2, 2, 2, 4, 4, 4, 2, 16, 32)  11.9 us
    reshape x1, local copies, waits for them, and re-layouts, step_three_four(): third = third.reshape(512, 1024)  8.54 us
    reshape x2, local copies, waits for them, and re-layouts, finish(): return moved.transpose(7, 9, 4, 1, 6, 8, 2, 5, 3, 0).reshape(512, 1024)  7.24 us
    transpose x1, local copies, waits for them, and re-layouts, step_three_four(): fourth.reshape(2, 2, 4, 2, 16, 2, 2, 2, 4, 32)  6.6 us
    transpose x1, local copies, waits for them, and re-layouts, finish(): return moved.transpose(7, 9, 4, 1, 6, 8, 2, 5, 3, 0).reshape(512, 1024)  5.29 us
  transfers between devices with their start and end apart: 1, of which 1 were waited for; matrix products, arithmetic and copies ran while one was open for 3% of the time, Pallas kernels for 0%

profile of v1, /device:TPU:1, one launch (start us, length us, event | category | flops | bytes accessed | tf_op | source)
XLA Modules:
  0.0 177.5 jit_solution(2844776680674504653)
XLA Ops:
  0.0 2.1 %fusion.1 = bf16[2,512,512]{2,1,0:T(8,128)(2,1)S(1)} fusion(bf16[64,2,8,512]{3,2,1,0:T(8,128)(2,1)} %bitcast.68, bf16[4,512,512]{2,1,0:T(8,128)(2,1)} %param.4), kind=kOutput, calls=%fused_computation.7 | convolution fusion | flops 537395200 | bytes 2621440 | tf_op jit(solution)/shard_map/dav,wv->awd/dot_general | solution.py:51
  2.1 0.3 reshape.90
  2.4 0.0 copy-start
  2.4 1.6 copy.47
  4.1 21.0 %all-to-all-start = ((bf16[128,32,128]{2,1,0:T(8,128)(2,1)}), bf16[128,32,128]{2,1,0:T(8,128)(2,1)S(1)}, u32[]{:S(2)}, u32[]{:S(2)}) async-start(bf16[128,32,128]{2,1,0:T(8,128)(2,1)} %bitcast.4), calls=%async_computation | async-start | bytes 2097152 | tf_op jit(solution)/shard_map/all_to_all | solution.py:18
  25.1 0.0 copy-done
  25.1 0.1 or_bitcast_fusion
  25.2 3.5 %negate_exponential_fusion = f32[512,1024]{1,0:T(8,128)} fusion(s32[1024]{0:T(1024)S(1)} %or_bitcast_fusion, f32[14]{0:T(128)S(1)} %convert_multiply_fusion, s32[512]{0:T(512)S(1)} %shift-left_or_fusion), kind=kOutput, calls=%fused_computation.3 | convolution fusion | flops 88676352 | bytes 2103352 | tf_op jit(solution)/shard_map/dot_general | solution.py:46
  28.7 1.9 %copy.50 = f32[512,1024]{0,1:T(8,128)S(1)} copy(f32[512,1024]{1,0:T(8,128)} %negate_exponential_fusion) | data formatting | bytes 4194304 | tf_op jit(solution)/shard_map/exp | solution.py:47
  30.6 29.6 %all-to-all-done = bf16[128,32,128]{2,1,0:T(8,128)(2,1)S(1)} async-done(((bf16[128,32,128]{2,1,0:T(8,128)(2,1)}), bf16[128,32,128]{2,1,0:T(8,128)(2,1)S(1)}, u32[]{:S(2)}, u32[]{:S(2)}) %all-to-all-start) | async-done | bytes 1048608 | tf_op jit(solution)/shard_map/all_to_all | solution.py:18
  60.2 0.1 copy.48
  60.3 1.8 %fusion = bf16[8,512,128]{1,2,0:T(8,128)(2,1)S(1)} fusion(f32[8,512,128]{1,2,0:T(8,128)S(1)} %bitcast.61, bf16[8,512,128]{2,1,0:T(8,128)(2,1)S(1)} %bitcast.66, bf16[4,512,512]{2,1,0:T(8,128)(2,1)} %param.4), kind=kOutput, calls=%fused_computation.2 | convolution fusion | flops 537919488 | bytes 4718592 | tf_op jit(solution)/shard_map/kj,gjl->gkl/dot_general | solution.py:60
  62.1 0.8 copy.51
  62.9 0.7 copy.52
  63.6 0.3 copy.53
  63.9 16.2 %all_to_all.15 = bf16[16,256,128]{2,1,0:T(8,128)(2,1)S(1)} all-to-all(bf16[16,256,128]{2,1,0:T(8,128)(2,1)S(1)} %copy.53), channel_id=1, replica_groups=mesh['zh'=2,'core'=2,'x'=4,'z1'=2,'z0'=2,'yh'=4,'y0'=2] {'x','z0','y0'}, dimensions={0} | all-to-all | bytes 2097152 | tf_op jit(solution)/shard_map/all_to_all | solution.py:18
  80.0 0.5 copy.54
  80.6 1.8 %convolution_convert_fusion.1 = bf16[1024,512]{1,0:T(8,128)(2,1)S(1)} fusion(bf16[1024,512]{0,1:T(8,128)(2,1)S(1)} %bitcast.67, bf16[4,512,512]{2,1,0:T(8,128)(2,1)} %param.4), kind=kOutput, calls=%fused_computation.5 | convolution fusion | flops 537395200 | bytes 2621440 | tf_op jit(solution)/shard_map/nd,ed->ne/dot_general | solution.py:68
  82.4 3.8 %reshape.99 = bf16[2,2,2,4,4,4,2,16,32]{8,7,6,5,4,3,2,1,0:T(8,128)(2,1)} reshape(bf16[1024,512]{1,0:T(8,128)(2,1)S(1)} %convolution_convert_fusion.1) | data formatting | bytes 2097152 | tf_op jit(solution)/shard_map/reshape | solution.py:70
  86.2 8.1 %copy.67 = bf16[2,2,2,4,4,4,2,16,32]{8,4,6,5,7,1,3,0,2:T(4,128)(2,1)} copy(bf16[2,2,2,4,4,4,2,16,32]{8,7,6,5,4,3,2,1,0:T(8,128)(2,1)} %reshape.99) | data formatting | bytes 2097152 | tf_op jit(solution)/shard_map/reshape | solution.py:70
  94.3 8.5 %reshape.100 = bf16[512,1024]{1,0:T(8,128)(2,1)S(1)} reshape(bf16[2,2,4,2,16,4,2,4,32]{8,7,6,5,4,3,2,1,0:T(4,128)(2,1)} %bitcast.58) | data formatting | bytes 2097152 | tf_op jit(solution)/shard_map/reshape | solution.py:71
  102.8 1.8 %fusion.2 = bf16[512,1024]{0,1:T(8,128)(2,1)S(1)} fusion(bf16[512,1024]{1,0:T(8,128)(2,1)S(1)} %reshape.100, bf16[4,512,512]{2,1,0:T(8,128)(2,1)} %param.4), kind=kOutput, calls=%fused_computation.8 | convolution fusion | flops 537395200 | bytes 2621440 | tf_op jit(solution)/shard_map/gh,hn->gn/dot_general | solution.py:72
  104.6 0.5 copy.56
  105.2 4.4 %reshape.101 = bf16[2,2,4,2,16,2,2,2,4,32]{9,8,7,6,5,4,3,2,1,0:T(4,128)(2,1)} reshape(bf16[512,1024]{1,0:T(8,128)(2,1)S(1)} %copy.56) | data formatting | bytes 2097152 | tf_op jit(solution)/shard_map/reshape | solution.py:74
  109.5 6.6 %copy.57 = bf16[4,2,2,2,2,2,2,16,4,32]{9,8,7,6,5,4,3,2,1,0:T(4,128)(2,1)} copy(bf16[4,2,2,2,2,2,2,16,4,32]{9,8,6,5,2,7,1,0,4,3:T(4,128)(2,1)} %bitcast.59) | data formatting | bytes 2097152 | tf_op jit(solution)/shard_map/transpose | solution.py:74
  116.1 5.2 %reshape.102 = bf16[128,32,128]{2,1,0:T(8,128)(2,1)S(1)} reshape(bf16[4,2,2,2,2,2,2,16,4,32]{9,8,7,6,5,4,3,2,1,0:T(4,128)(2,1)} %copy.57) | data formatting | bytes 2097152 | tf_op jit(solution)/shard_map/reshape | solution.py:75
  121.4 40.3 %all_to_all.16 = bf16[128,32,128]{2,1,0:T(8,128)(2,1)S(1)} all-to-all(bf16[128,32,128]{2,1,0:T(8,128)(2,1)S(1)} %reshape.102), channel_id=1, replica_groups=mesh['zh'=2,'core'=2,'x'=4,'z1'=2,'z0'=2,'yh'=4,'y0'=2] {'yh','y0','zh',..., dimensions={0} | all-to-all | bytes 2097152 | tf_op jit(solution)/shard_map/all_to_all | solution.py:18
  161.7 3.2 %reshape.103 = bf16[4,2,2,2,2,2,2,16,4,32]{9,8,7,6,5,4,3,2,1,0:T(4,128)(2,1)} reshape(bf16[128,32,128]{2,1,0:T(8,128)(2,1)S(1)} %all_to_all.16) | data formatting | bytes 2097152 | tf_op jit(solution)/shard_map/reshape | solution.py:79
  164.9 5.3 %copy.58 = bf16[16,32,2,2,2,4,2,2,2,4]{1,0,9,8,7,6,5,4,3,2:T(8,128)(2,1)} copy(bf16[16,32,2,2,2,4,2,2,2,4]{1,5,0,4,7,2,8,6,3,9:T(4,128)(2,1)} %bitcast.60) | data formatting | bytes 2097152 | tf_op jit(solution)/shard_map/transpose | solution.py:80
  170.2 5.9 %reshape.104 = bf16[512,1024]{0,1:T(8,128)(2,1)S(1)} reshape(bf16[16,32,2,2,2,4,2,2,2,4]{1,0,9,8,7,6,5,4,3,2:T(8,128)(2,1)} %copy.58) | data formatting | bytes 2097152 | tf_op jit(solution)/shard_map/reshape | solution.py:80
  176.1 1.3 copy.59
  (3 shorter events, 0.0 us)
Async XLA Ops:
  2.4 22.7 %copy-start = (s32[14]{0:T(128)S(1)}, s32[14]{0:T(128)}, u32[]{:S(2)}) copy-start(s32[14]{0:T(128)} %param.5) | copy-start | bytes 172
  4.1 56.1 %all-to-all-start = ((bf16[128,32,128]{2,1,0:T(8,128)(2,1)}), bf16[128,32,128]{2,1,0:T(8,128)(2,1)S(1)}, u32[]{:S(2)}, u32[]{:S(2)}) async-start(bf16[128,32,128]{2,1,0:T(8,128)(2,1)} %bitcast.4), calls=%async_computation | async-start | bytes 2097152 | tf_op jit(solution)/shard_map/all_to_all | solution.py:18

commit v2 on v1

v2 whole, which is shorter than its diff:
```python
import jax
import jax.numpy as jnp
from jax import lax
from jax.experimental import pallas as pl
from jax.experimental.pallas import tpu as pltpu
from jax.sharding import Mesh, PartitionSpec as P

BLOCK = 512
SITES = 14
COUPLING = 0.06

AXES = ("zh", "core", "x", "z1", "z0", "yh", "y0")
SIZES = (2, 2, 4, 2, 2, 4, 2)
EX1 = ("zh", "core", "x", "z1", "yh")
EX2 = ("x", "z0", "y0")
EX3 = ("yh", "y0", "zh", "z1", "z0", "core")

NT = (((1,), (1,)), ((), ()))
NN = (((1,), (0,)), ((), ()))


def exchange(value, axes):
    return lax.all_to_all(value, axes, split_axis=0, concat_axis=0, tiled=True)


def product(left, right, dims):
    return lax.dot_general(left, right, dims, preferred_element_type=jnp.float32)


def swap_groups(parts):
    lane = lax.broadcasted_iota(jnp.int32, parts[0].shape, 1)
    low_half = lane < 64
    low_quarter = (lane & 32) == 0
    half = [None] * 4
    for j in range(2):
        low, high = parts[j], parts[j + 2]
        half[j] = jnp.where(low_half, low, pltpu.roll(high, 64, 1))
        half[j + 2] = jnp.where(low_half, pltpu.roll(low, 64, 1), high)
    out = [None] * 4
    for j in (0, 2):
        low, high = half[j], half[j + 1]
        out[j] = jnp.where(low_quarter, low, pltpu.roll(high, 32, 1))
        out[j + 1] = jnp.where(low_quarter, pltpu.roll(low, 96, 1), high)
    return out


def permuted_rows(matrix, source):
    row = lax.broadcasted_iota(jnp.int32, (BLOCK, BLOCK), 0)
    col = lax.broadcasted_iota(jnp.int32, (BLOCK, BLOCK), 1)
    pick = jnp.where(col == source(row), 1.0, 0.0).astype(jnp.bfloat16)
    return product(pick, matrix, NN).astype(jnp.bfloat16)


def first_kernel(x_ref, hop_ref, out_ref, rows_ref):
    @pl.when(pl.program_id(0) == 0)
    def _():
        rows_ref[...] = permuted_rows(hop_ref[0], lambda r: ((r & 15) << 5) | (r >> 4))

    first = product(rows_ref[...], x_ref[...], NT).astype(jnp.bfloat16)
    for x in range(4):
        out_ref[:, x] = first[:, x * 128 : (x + 1) * 128].reshape(4, 8, 16, 128)


def step_one(amplitudes, hop_blocks):
    out = pl.pallas_call(
        first_kernel,
        grid=(2,),
        in_specs=[
            pl.BlockSpec((512, 512), lambda a: (0, a)),
            pl.BlockSpec((1, 512, 512), lambda a: (0, 0, 0)),
        ],
        out_specs=pl.BlockSpec((4, 4, 8, 16, 128), lambda a: (0, 0, 0, a, 0)),
        out_shape=jax.ShapeDtypeStruct((4, 4, 8, 32, 128), jnp.bfloat16),
        scratch_shapes=[pltpu.VMEM((512, 512), jnp.bfloat16)],
        cost_estimate=pl.CostEstimate(
            flops=2 * 512 * 512 * 1536, bytes_accessed=5 << 19, transcendentals=0
        ),
        name="first",
    )(amplitudes, hop_blocks)
    return out.reshape(128, 32, 128)


def prepare_kernel(seed_ref, dev_ref, hop_ref, rows_ref, base_ref, side_ref):
    def source(r):
        return (
            ((r & 4) << 6)
            | ((r & 2) << 6)
            | ((r >> 2) & 0x78)
            | ((r & 1) << 2)
            | ((r >> 3) & 3)
        )

    rows_ref[...] = permuted_rows(hop_ref[0], source)
    cost = [COUPLING * seed_ref[i].astype(jnp.float32) for i in range(SITES)]
    place = dev_ref[0]

    def at(shift):
        return ((place >> shift) & 1).astype(jnp.float32)

    zh, core, x1, x0, z1, z0, y2, y1, y0 = [at(8 - b) for b in range(9)]
    row = lax.broadcasted_iota(jnp.int32, (BLOCK, 128), 0)
    lane = lax.broadcasted_iota(jnp.int32, (BLOCK, 128), 1)

    def bit(index, shift):
        return ((index >> shift) & 1).astype(jnp.float32)

    energy = (cost[12] * z0) * bit(row, 1) + (cost[9] * y0) * bit(row, 6)
    energy += (cost[8] * x1) * bit(row, 5) + (cost[7] * x0) * bit(row, 0)
    energy += cost[6] * (bit(row, 4) * bit(lane, 6)) + cost[5] * (bit(row, 3) * bit(lane, 5))
    for site, held in enumerate((y1, y2, z1, core, zh)):
        energy += (cost[site] * held) * bit(lane, site)
    base_ref[...] = jnp.exp(-energy)
    small = lax.broadcasted_iota(jnp.int32, (8, 128), 0)
    for g in range(8):
        for top in range(4):
            extra = bit(small, 2) * (cost[13] * float(g >> 2))
            extra += cost[11] * float(((g >> 1) & 1) * (top >> 1))
            extra += cost[10] * float((g & 1) * (top & 1))
            side_ref[g, top] = jnp.exp(-extra)


def prepare(hop_blocks, coupling_seed):
    place = lax.axis_index(AXES).astype(jnp.int32).reshape(1)
    smem = pl.BlockSpec(memory_space=pltpu.SMEM)
    return pl.pallas_call(
        prepare_kernel,
        grid=(1,),
        in_specs=[smem, smem, pl.BlockSpec((1, 512, 512), lambda i: (1, 0, 0))],
        out_specs=[
            pl.BlockSpec((512, 512), lambda i: (0, 0)),
            pl.BlockSpec((512, 128), lambda i: (0, 0)),
            pl.BlockSpec((8, 4, 8, 128), lambda i: (0, 0, 0, 0)),
        ],
        out_shape=[
            jax.ShapeDtypeStruct((512, 512), jnp.bfloat16),
            jax.ShapeDtypeStruct((512, 128), jnp.float32),
            jax.ShapeDtypeStruct((8, 4, 8, 128), jnp.float32),
        ],
        cost_estimate=pl.CostEstimate(
            flops=2 * 512 * 512 * 512, bytes_accessed=3 << 19, transcendentals=1 << 17
        ),
        name="prepare",
    )(coupling_seed, place, hop_blocks)


def second_kernel(moved_ref, rows_ref, base_ref, side_ref, out_ref):
    data = jnp.concatenate([moved_ref[:, g].reshape(512, 128) for g in range(4)], axis=1)
    second = product(rows_ref[...], data, NN)
    base = base_ref[...].reshape(4, 16, 8, 128)
    for g in range(4):
        part = second[:, g * 128 : (g + 1) * 128].reshape(4, 16, 8, 128)
        mixed = part * (base * side_ref[g][:, None])
        out_ref[:, g] = mixed.reshape(16, 32, 128).astype(jnp.bfloat16)


def step_two(moved, rows, base, side):
    out = pl.pallas_call(
        second_kernel,
        grid=(2,),
        in_specs=[
            pl.BlockSpec((16, 4, 32, 128), lambda i: (0, i, 0, 0)),
            pl.BlockSpec((512, 512), lambda i: (0, 0)),
            pl.BlockSpec((512, 128), lambda i: (0, 0)),
            pl.BlockSpec((4, 4, 8, 128), lambda i: (i, 0, 0, 0)),
        ],
        out_specs=pl.BlockSpec((16, 4, 32, 128), lambda i: (0, i, 0, 0)),
        out_shape=jax.ShapeDtypeStruct((16, 8, 32, 128), jnp.bfloat16),
        cost_estimate=pl.CostEstimate(
            flops=2 * 512 * 512 * 1024, bytes_accessed=3 << 20, transcendentals=0
        ),
        name="second",
    )(moved.reshape(16, 8, 32, 128), rows, base, side)
    return out.reshape(16, 256, 128)


def third_kernel(moved_ref, low_ref, high_ref, out_ref, held_ref):
    step = pl.program_id(0)

    @pl.when(step < 4)
    def _():
        data = jnp.concatenate([moved_ref[x, 0] for x in range(4)], axis=1)
        third = product(data, low_ref[0], NT)
        at = (step >> 1) * 128 + (step & 1) * 16
        for top in range(4):
            lanes = slice(top * 128, (top + 1) * 128)
            parts = [
                jnp.concatenate(
                    [third[(g * 4 + j) * 8 : (g * 4 + j) * 8 + 8, lanes] for g in range(8)], axis=0
                )
                for j in range(4)
            ]
            swapped = swap_groups(parts)
            for j in range(4):
                for g in range(8):
                    where = at + (g >> 2) * 256 + (g & 3) * 32 + top * 4 + j
                    held_ref[pl.ds(pl.multiple_of(where * 8, 8), 8), :] = swapped[j][
                        g * 8 : g * 8 + 8
                    ]

    @pl.when(step >= 4)
    def _():
        s = (step - 4) * 2
        data = jnp.concatenate(
            [held_ref[pl.ds(s + b, 512, stride=8), :].astype(jnp.bfloat16) for b in range(2)],
            axis=1,
        )
        fourth = product(high_ref[0], data, NN).astype(jnp.bfloat16)
        for b in range(2):
            for r in range(32):
                d13, d12, mid, d9 = r >> 4, (r >> 3) & 1, (r >> 1) & 3, r & 1
                out_ref[mid, d9, 0, d13, d12, 0, b] = fourth[
                    r * 16 : r * 16 + 16, b * 128 : (b + 1) * 128
                ]


def step_three_four(moved, hop_blocks):
    out = pl.pallas_call(
        third_kernel,
        grid=(8,),
        in_specs=[
            pl.BlockSpec((4, 1, 256, 128), lambda i: (0, jnp.minimum(i, 3), 0, 0)),
            pl.BlockSpec((1, 512, 512), lambda i: (2, 0, 0)),
            pl.BlockSpec((1, 512, 512), lambda i: (3, 0, 0)),
        ],
        out_specs=pl.BlockSpec(
            (4, 2, 1, 2, 2, 1, 2, 16, 128),
            lambda i: (
                0,
                0,
                jnp.maximum(i - 4, 0) // 2,
                0,
                0,
                jnp.maximum(i - 4, 0) % 2,
                0,
                0,
                0,
            ),
        ),
        out_shape=jax.ShapeDtypeStruct((4, 2, 2, 2, 2, 2, 2, 16, 128), jnp.bfloat16),
        scratch_shapes=[pltpu.VMEM((4096, 128), jnp.float32)],
        cost_estimate=pl.CostEstimate(
            flops=4 * 512 * 512 * 1024, bytes_accessed=3 << 20, transcendentals=0
        ),
        name="third",
    )(moved.reshape(4, 4, 256, 128), hop_blocks, hop_blocks)
    return out.reshape(128, 32, 128)


def last_kernel(moved_ref, out_ref, held_ref):
    for low in range(32):
        u4, u3, u2, u10 = low >> 4, (low >> 3) & 1, (low >> 2) & 1, low & 3
        block = moved_ref[u10, 0, u4, u2, 0, u3].astype(jnp.float32)
        for u7 in range(2):
            held_ref[(u7 * 32 + low) * 16 : (u7 * 32 + low + 1) * 16, :] = block[
                u7 * 16 : u7 * 16 + 16
            ]
    for u7 in range(2):
        for top in range(4):
            parts = [
                held_ref[pl.ds(u7 * 512 + top * 4 + j, 32, stride=16), :] for j in range(4)
            ]
            tile = jnp.concatenate(swap_groups(parts), axis=0)
            out_ref[top * 128 : (top + 1) * 128, u7 * 128 : (u7 + 1) * 128] = tile.T.astype(
                jnp.bfloat16
            )


def finish(moved):
    return pl.pallas_call(
        last_kernel,
        grid=(4,),
        in_specs=[
            pl.BlockSpec(
                (4, 1, 2, 2, 1, 2, 32, 128), lambda i: (0, i % 2, 0, 0, i // 2, 0, 0, 0)
            )
        ],
        out_specs=pl.BlockSpec((512, 256), lambda i: (0, i)),
        out_shape=jax.ShapeDtypeStruct((512, 1024), jnp.bfloat16),
        scratch_shapes=[pltpu.VMEM((1024, 128), jnp.float32)],
        name="last",
    )(moved.reshape(4, 2, 2, 2, 2, 2, 32, 128))


def on_device(amplitudes, hop_blocks, coupling_seed):
    rows, base, side = prepare(hop_blocks, coupling_seed)
    sent = exchange(step_one(amplitudes, hop_blocks), EX1)
    sent = exchange(step_two(sent, rows, base, side), EX2)
    sent = exchange(step_three_four(sent, hop_blocks), EX3)
    return finish(sent)


def solution(mesh):
    fine = Mesh(mesh.devices.reshape(SIZES), AXES)
    spec = P(("z1", "z0", "yh", "y0"), ("zh", "core", "x"))
    return jax.shard_map(
        on_device, mesh=fine, in_specs=(spec, P(), P()), out_specs=spec, check_vma=False
    )
```

time: 178 us -> 134 us (0.75)
  local copies, waits for them, and re-layouts: 59.1 us -> 0.97 us
  Pallas kernels: 0 us -> 20.8 us
  matrix products: 11 us -> 0 us
  waiting for transfers between devices: 29.6 us -> 32.5 us
  blocking collectives: 56.5 us -> 58.5 us
    reshape x11 -> x0, local copies, waits for them, and re-layouts: 42.7 us -> none  [the longest x2 11.9 us: step_three_four(): third.reshape(2, 2, 2, 4, 4, 4, 2, 16, 32)]
    pallas_call x0 -> x5, Pallas kernels: none -> 20.8 us  [the longest x1 6.72 us: step_three_four(): pl.pallas_call(third_kernel, grid=(8,), in_specs=[pl.BlockSpec((4, 1, 256...]
    transpose x5 -> x0, local copies, waits for them, and re-layouts: 13.2 us -> none  [the longest x1 6.6 us: step_three_four(): fourth.reshape(2, 2, 4, 2, 16, 2, 2, 2, 4, 32)]
    dot_general x5 -> x0, matrix products: 11 us -> none  [the longest x1 3.46 us: interaction(): energy = jnp.dot(nu * c, nd.T, precision=lax.Precision.HIGHEST)]
    all_to_all x1, waiting for transfers between devices: 29.6 us -> 32.5 us  [exchange(): return lax.all_to_all(value, axes, split_axis=0, concat_axis=0, tiled=True)]
    all_to_all x2, blocking collectives: 56.5 us -> 58.5 us  [exchange(): return lax.all_to_all(value, axes, split_axis=0, concat_axis=0, tiled=True)]
    exp x1 -> x0, local copies, waits for them, and re-layouts: 1.92 us -> none  [interaction(): return jnp.exp(-energy).reshape(BLOCK, 8, 128).transpose(1, 0, 2)]
  transfers between devices with their start and end apart: 1 -> 1, of which waited for: 1 -> 1; matrix products, arithmetic and copies ran while one was open for 3% -> 0% of each run, Pallas kernels for 0% -> 2%
where the time goes in v2:
time: 134 us
  blocking collectives  58.5 us (44%)
  waiting for transfers between devices  32.5 us (24%)
  starting transfers between devices  21 us (16%)
  Pallas kernels  20.8 us (16%)
    all_to_all x2, blocking collectives, exchange(): return lax.all_to_all(value, axes, split_axis=0, concat_axis=0, tiled=True)  58.5 us
    all_to_all x1, waiting for transfers between devices, exchange(): return lax.all_to_all(value, axes, split_axis=0, concat_axis=0, tiled=True)  32.5 us
    all_to_all x1, starting transfers between devices, exchange(): return lax.all_to_all(value, axes, split_axis=0, concat_axis=0, tiled=True)  21 us
    pallas_call x1, Pallas kernels, step_three_four(): pl.pallas_call(third_kernel, grid=(8,), in_specs=[pl.BlockSpec((4, 1, 256...  6.72 us
    pallas_call x1, Pallas kernels, finish(): pl.pallas_call(last_kernel, grid=(4,), in_specs=[pl.BlockSpec((4, 1, 2, 2...  5.03 us
    pallas_call x1, Pallas kernels, step_one(): pl.pallas_call(first_kernel, grid=(2,), in_specs=[pl.BlockSpec((512, 512)...  3.41 us
    pallas_call x1, Pallas kernels, step_two(): pl.pallas_call(second_kernel, grid=(2,), in_specs=[pl.BlockSpec((16, 4, 3...  3.01 us
  transfers between devices with their start and end apart: 1, of which 1 were waited for; matrix products, arithmetic and copies ran while one was open for 0% of the time, Pallas kernels for 2%

profile of v2, /device:TPU:1, one launch (start us, length us, event | category | flops | bytes accessed | tf_op | source)
XLA Modules:
  0.0 133.8 jit_solution(16882790898169344550)
XLA Ops:
  0.0 3.4 %first.1 = bf16[4,4,8,32,128]{4,3,2,1,0:T(8,128)(2,1)} custom-call(bf16[512,1024]{1,0:T(8,128)(2,1)} %x_ref.1, bf16[4,512,512]{2,1,0:T(8,128)(2,1)} %high_ref.1), custom_call_target="tpu_custom_call" | custom-call | flops 805306368 | bytes 2621440 | tf_op jit(solution)/shard_map/first/pallas_call | solution.py:65
  3.4 21.0 %all-to-all-start = ((bf16[128,32,128]{2,1,0:T(8,128)(2,1)}), bf16[128,32,128]{2,1,0:T(8,128)(2,1)S(1)}, u32[]{:S(2)}, u32[]{:S(2)}) async-start(bf16[128,32,128]{2,1,0:T(8,128)(2,1)} %bitcast.10), calls=%async_computation | async-start | bytes 2097152 | tf_op jit(solution)/shard_map/all_to_all | solution.py:23
  24.4 2.6 %prepare.1 = (bf16[512,512]{1,0:T(8,128)(2,1)}, f32[512,128]{1,0:T(8,128)}, f32[8,4,8,128]{3,2,1,0:T(8,128)}) custom-call(s32[14]{0:T(128)} %seed_ref.1, s32[1]{0:T(128)} %bitcast.2.dev_ref, bf16[4,512,512]{2,1,0:T(8,128)(2,1)} %high_ref.1), custom_call_target="tpu_custom_call" | custom-call | flops 268435456 | bytes 1572864 | tf_op jit(solution)/shard_map/prepare/pallas_call | solution.py:125
  27.0 32.5 %all-to-all-done = bf16[128,32,128]{2,1,0:T(8,128)(2,1)S(1)} async-done(((bf16[128,32,128]{2,1,0:T(8,128)(2,1)}), bf16[128,32,128]{2,1,0:T(8,128)(2,1)S(1)}, u32[]{:S(2)}, u32[]{:S(2)}) %all-to-all-start) | async-done | bytes 1048608 | tf_op jit(solution)/shard_map/all_to_all | solution.py:23
  59.5 0.0 copy-start
  59.6 1.0 copy-done
  60.5 3.0 %second.1 = bf16[16,8,32,128]{3,2,1,0:T(8,128)(2,1)} custom-call(bf16[16,8,32,128]{3,2,1,0:T(8,128)(2,1)} %bitcast.7, bf16[512,512]{1,0:T(8,128)(2,1)} %get-tuple-element.8.rows_ref, f32[512,128]{1,0:T(8,128)} %get-tuple-element.9.base_ref, f32[8,4,8,128]{3,2,1,0:T(8,128)} %get-tuple-element.10.side_ref), custom_call_target="tpu_custom_call" | custom-call | flops 536870912 | bytes 3145728 | tf_op jit(solution)/shard_map/second/pallas_call | solution.py:157
  63.5 18.2 %all_to_all.15 = bf16[16,256,128]{2,1,0:T(8,128)(2,1)} all-to-all(bf16[16,256,128]{2,1,0:T(8,128)(2,1)} %bitcast.8), channel_id=1, replica_groups=mesh['zh'=2,'core'=2,'x'=4,'z1'=2,'z0'=2,'yh'=4,'y0'=2] {'x','z0','y0'}, dimensions={0} | all-to-all | bytes 2097152 | tf_op jit(solution)/shard_map/all_to_all | solution.py:23
  81.7 6.7 %third.1 = bf16[4,2,2,2,2,2,2,16,128]{8,7,6,5,4,3,2,1,0:T(8,128)(2,1)} custom-call(bf16[4,4,256,128]{3,2,1,0:T(8,128)(2,1)} %bitcast.11, bf16[4,512,512]{2,1,0:T(8,128)(2,1)} %high_ref.1, bf16[4,512,512]{2,1,0:T(8,128)(2,1)} %high_ref.1), custom_call_target="tpu_custom_call" | custom-call | flops 1073741824 | bytes 3145728 | tf_op jit(solution)/shard_map/third/pallas_call | solution.py:217
  88.4 40.3 %all_to_all.16 = bf16[128,32,128]{2,1,0:T(8,128)(2,1)} all-to-all(bf16[128,32,128]{2,1,0:T(8,128)(2,1)} %bitcast.12), channel_id=1, replica_groups=mesh['zh'=2,'core'=2,'x'=4,'z1'=2,'z0'=2,'yh'=4,'y0'=2] {'yh','y0','zh',..., dimensions={0} | all-to-all | bytes 2097152 | tf_op jit(solution)/shard_map/all_to_all | solution.py:23
  128.7 5.0 %last.1 = bf16[512,1024]{1,0:T(8,128)(2,1)} custom-call(bf16[4,2,2,2,2,2,32,128]{7,6,5,4,3,2,1,0:T(8,128)(2,1)} %bitcast.9), custom_call_target="tpu_custom_call" | custom-call | tf_op jit(solution)/shard_map/last/pallas_call | solution.py:269
Async XLA Ops:
  3.4 56.1 %all-to-all-start = ((bf16[128,32,128]{2,1,0:T(8,128)(2,1)}), bf16[128,32,128]{2,1,0:T(8,128)(2,1)S(1)}, u32[]{:S(2)}, u32[]{:S(2)}) async-start(bf16[128,32,128]{2,1,0:T(8,128)(2,1)} %bitcast.10), calls=%async_computation | async-start | bytes 2097152 | tf_op jit(solution)/shard_map/all_to_all | solution.py:23
  59.5 1.0 copy-start

commit v3 on v2

v3 whole, which is shorter than its diff:
```python
import jax
import jax.numpy as jnp
from jax import lax
from jax.experimental import pallas as pl
from jax.experimental.pallas import tpu as pltpu
from jax.sharding import Mesh, PartitionSpec as P

BLOCK = 512
SITES = 14
COUPLING = 0.06

AXES = ("zh", "core", "x", "z1", "z0", "yh", "y0")
SIZES = (2, 2, 4, 2, 2, 4, 2)
EX1 = ("zh", "core", "x", "z1", "yh")
EX2 = ("x", "z0", "y0")
EX3 = ("yh", "y0", "zh", "z1", "z0", "core")

NT = (((1,), (1,)), ((), ()))
NN = (((1,), (0,)), ((), ()))


def exchange(value, axes):
    return lax.all_to_all(value, axes, split_axis=0, concat_axis=0, tiled=True)


def product(left, right, dims):
    return lax.dot_general(left, right, dims, preferred_element_type=jnp.float32)


def swap_groups(parts):
    group = lax.broadcasted_iota(jnp.int32, parts[0].shape, 1) >> 5
    is_group = [group == q for q in range(3)]

    def choose(values):
        out = values[3]
        for q in range(3):
            out = jnp.where(is_group[q], values[q], out)
        return out

    turned = []
    for m in range(4):
        held = choose([parts[(q + m) & 3] for q in range(4)])
        turned.append(held if m == 0 else pltpu.roll(held, 32 * m, 1))
    return [choose([turned[(q - a) & 3] for q in range(4)]) for a in range(4)]


def permuted_rows(matrix, source):
    row = lax.broadcasted_iota(jnp.int32, (BLOCK, BLOCK), 0)
    col = lax.broadcasted_iota(jnp.int32, (BLOCK, BLOCK), 1)
    pick = jnp.where(col == source(row), 1.0, 0.0).astype(jnp.bfloat16)
    return product(pick, matrix, NN).astype(jnp.bfloat16)


def first_kernel(x_ref, hop_ref, out_ref, rows_ref):
    rows = permuted_rows(hop_ref[0], lambda r: ((r & 15) << 5) | (r >> 4))
    for u9 in range(2):
        first = product(rows, x_ref[:, u9 * 512 : (u9 + 1) * 512], NT).astype(jnp.bfloat16)
        for x in range(4):
            out_ref[:, x, :, u9 * 16 : (u9 + 1) * 16] = first[:, x * 128 : (x + 1) * 128].reshape(
                4, 8, 16, 128
            )


def step_one(amplitudes, hop_blocks):
    out = pl.pallas_call(
        first_kernel,
        grid=(1,),
        in_specs=[
            pl.BlockSpec((512, 1024), lambda i: (0, 0)),
            pl.BlockSpec((1, 512, 512), lambda i: (0, 0, 0)),
        ],
        out_specs=pl.BlockSpec((4, 4, 8, 32, 128), lambda i: (0, 0, 0, 0, 0)),
        out_shape=jax.ShapeDtypeStruct((4, 4, 8, 32, 128), jnp.bfloat16),
        scratch_shapes=[pltpu.VMEM((8, 128), jnp.float32)],
        cost_estimate=pl.CostEstimate(
            flops=2 * 512 * 512 * 1536, bytes_accessed=5 << 19, transcendentals=0
        ),
        name="first",
        compiler_params=pltpu.CompilerParams(vmem_limit_bytes=16 << 20),
    )(amplitudes, hop_blocks[:1])
    return out.reshape(128, 32, 128)


def prepare_kernel(seed_ref, dev_ref, hop_ref, rows_ref, base_ref, side_ref):
    def source(r):
        return (
            ((r & 4) << 6)
            | ((r & 2) << 6)
            | ((r >> 2) & 0x78)
            | ((r & 1) << 2)
            | ((r >> 3) & 3)
        )

    rows_ref[...] = permuted_rows(hop_ref[0], source)
    cost = [COUPLING * seed_ref[i].astype(jnp.float32) for i in range(SITES)]
    place = dev_ref[0]

    def at(shift):
        return ((place >> shift) & 1).astype(jnp.float32)

    zh, core, x1, x0, z1, z0, y2, y1, y0 = [at(8 - b) for b in range(9)]
    row = lax.broadcasted_iota(jnp.int32, (BLOCK, 128), 0)
    lane = lax.broadcasted_iota(jnp.int32, (BLOCK, 128), 1)

    def bit(index, shift):
        return ((index >> shift) & 1).astype(jnp.float32)

    energy = (cost[12] * z0) * bit(row, 1) + (cost[9] * y0) * bit(row, 6)
    energy += (cost[8] * x1) * bit(row, 5) + (cost[7] * x0) * bit(row, 0)
    energy += cost[6] * (bit(row, 4) * bit(lane, 6)) + cost[5] * (bit(row, 3) * bit(lane, 5))
    for site, held in enumerate((y1, y2, z1, core, zh)):
        energy += (cost[site] * held) * bit(lane, site)
    base_ref[...] = jnp.exp(-energy)
    small = lax.broadcasted_iota(jnp.int32, (8, 128), 0)
    for g in range(8):
        for top in range(4):
            extra = bit(small, 2) * (cost[13] * float(g >> 2))
            extra += cost[11] * float(((g >> 1) & 1) * (top >> 1))
            extra += cost[10] * float((g & 1) * (top & 1))
            side_ref[g, top] = jnp.exp(-extra)


def prepare(hop_blocks, coupling_seed):
    place = lax.axis_index(AXES).astype(jnp.int32).reshape(1)
    smem = pl.BlockSpec(memory_space=pltpu.SMEM)
    return pl.pallas_call(
        prepare_kernel,
        grid=(1,),
        in_specs=[smem, smem, pl.BlockSpec((1, 512, 512), lambda i: (1, 0, 0))],
        out_specs=[
            pl.BlockSpec((512, 512), lambda i: (0, 0)),
            pl.BlockSpec((512, 128), lambda i: (0, 0)),
            pl.BlockSpec((8, 4, 8, 128), lambda i: (0, 0, 0, 0)),
        ],
        out_shape=[
            jax.ShapeDtypeStruct((512, 512), jnp.bfloat16),
            jax.ShapeDtypeStruct((512, 128), jnp.float32),
            jax.ShapeDtypeStruct((8, 4, 8, 128), jnp.float32),
        ],
        cost_estimate=pl.CostEstimate(
            flops=2 * 512 * 512 * 512, bytes_accessed=3 << 19, transcendentals=1 << 17
        ),
        name="prepare",
        compiler_params=pltpu.CompilerParams(vmem_limit_bytes=16 << 20),
    )(coupling_seed, place, hop_blocks)


def second_kernel(moved_ref, rows_ref, base_ref, side_ref, out_ref):
    base = base_ref[...].reshape(4, 16, 8, 128)
    for half in range(4):
        data = jnp.concatenate(
            [moved_ref[:, half * 2 + g].reshape(512, 128) for g in range(2)], axis=1
        )
        second = product(rows_ref[...], data, NN)
        for b in range(2):
            g = half * 2 + b
            part = second[:, b * 128 : (b + 1) * 128].reshape(4, 16, 8, 128)
            mixed = part * (base * side_ref[g][:, None])
            out_ref[:, g] = mixed.reshape(16, 32, 128).astype(jnp.bfloat16)


def step_two(moved, rows, base, side):
    out = pl.pallas_call(
        second_kernel,
        grid=(1,),
        in_specs=[
            pl.BlockSpec((16, 8, 32, 128), lambda i: (0, i, 0, 0)),
            pl.BlockSpec((512, 512), lambda i: (0, 0)),
            pl.BlockSpec((512, 128), lambda i: (0, 0)),
            pl.BlockSpec((8, 4, 8, 128), lambda i: (i, 0, 0, 0)),
        ],
        out_specs=pl.BlockSpec((16, 8, 32, 128), lambda i: (0, i, 0, 0)),
        out_shape=jax.ShapeDtypeStruct((16, 8, 32, 128), jnp.bfloat16),
        cost_estimate=pl.CostEstimate(
            flops=2 * 512 * 512 * 1024, bytes_accessed=3 << 20, transcendentals=0
        ),
        name="second",
        compiler_params=pltpu.CompilerParams(vmem_limit_bytes=16 << 20),
    )(moved.reshape(16, 8, 32, 128), rows, base, side)
    return out.reshape(16, 256, 128)


def third_kernel(moved_ref, low_ref, high_ref, out_ref, held_ref):
    for step in range(4):
        data = jnp.concatenate([moved_ref[x, step] for x in range(4)], axis=1)
        third = product(data, low_ref[0], NT)
        at = (step >> 1) * 128 + (step & 1) * 16
        for top in range(4):
            lanes = slice(top * 128, (top + 1) * 128)
            parts = [
                jnp.concatenate(
                    [third[(g * 4 + j) * 8 : (g * 4 + j) * 8 + 8, lanes] for g in range(8)], axis=0
                )
                for j in range(4)
            ]
            swapped = swap_groups(parts)
            for j in range(4):
                for g in range(8):
                    where = (at + (g >> 2) * 256 + (g & 3) * 32 + top * 4 + j) * 8
                    held_ref[where : where + 8, :] = swapped[j][g * 8 : g * 8 + 8]
    for step in range(4):
        data = jnp.concatenate(
            [
                held_ref[pl.ds(step * 2 + b, 512, stride=8), :].astype(jnp.bfloat16)
                for b in range(2)
            ],
            axis=1,
        )
        fourth = product(high_ref[0], data, NN).astype(jnp.bfloat16)
        for b in range(2):
            for r in range(32):
                d13, d12, mid, d9 = r >> 4, (r >> 3) & 1, (r >> 1) & 3, r & 1
                out_ref[mid, d9, step >> 1, d13, d12, step & 1, b] = fourth[
                    r * 16 : r * 16 + 16, b * 128 : (b + 1) * 128
                ]


def step_three_four(moved, hop_blocks):
    out = pl.pallas_call(
        third_kernel,
        grid=(1,),
        in_specs=[
            pl.BlockSpec((4, 4, 256, 128), lambda i: (0, 0, 0, 0)),
            pl.BlockSpec((1, 512, 512), lambda i: (2, 0, 0)),
            pl.BlockSpec((1, 512, 512), lambda i: (3, 0, 0)),
        ],
        out_specs=pl.BlockSpec(
            (4, 2, 2, 2, 2, 2, 2, 16, 128), lambda i: (0, 0, 0, 0, 0, 0, 0, 0, 0)
        ),
        out_shape=jax.ShapeDtypeStruct((4, 2, 2, 2, 2, 2, 2, 16, 128), jnp.bfloat16),
        scratch_shapes=[pltpu.VMEM((4096, 128), jnp.float32)],
        cost_estimate=pl.CostEstimate(
            flops=4 * 512 * 512 * 1024, bytes_accessed=3 << 20, transcendentals=0
        ),
        name="third",
        compiler_params=pltpu.CompilerParams(vmem_limit_bytes=16 << 20),
    )(moved.reshape(4, 4, 256, 128), hop_blocks, hop_blocks)
    return out.reshape(128, 32, 128)


def last_kernel(moved_ref, out_ref, held_ref):
    row = lax.broadcasted_iota(jnp.int32, (128, 128), 0)
    col = lax.broadcasted_iota(jnp.int32, (128, 128), 1)
    eye = jnp.where(row == col, 1.0, 0.0).astype(jnp.bfloat16)
    for pair in range(2):
        u9, u8 = pair >> 1, pair & 1
        for low in range(32):
            u4, u3, u2, u10 = low >> 4, (low >> 3) & 1, (low >> 2) & 1, low & 3
            block = moved_ref[u10, u8, u4, u2, u9, u3].astype(jnp.float32)
            for u7 in range(2):
                at = ((pair * 2 + u7) * 32 + low) * 16
                held_ref[at : at + 16, :] = block[u7 * 16 : u7 * 16 + 16]
    for lane in range(4):
        for top in range(4):
            parts = [
                held_ref[pl.ds(lane * 512 + top * 4 + j, 32, stride=16), :] for j in range(4)
            ]
            tile = jnp.concatenate(swap_groups(parts), axis=0).astype(jnp.bfloat16)
            out_ref[top * 128 : (top + 1) * 128, lane * 128 : (lane + 1) * 128] = product(
                eye, tile, NT
            ).astype(jnp.bfloat16)


def finish(moved):
    return pl.pallas_call(
        last_kernel,
        grid=(2,),
        in_specs=[
            pl.BlockSpec((4, 2, 2, 2, 1, 2, 32, 128), lambda i: (0, 0, 0, 0, i, 0, 0, 0))
        ],
        out_specs=pl.BlockSpec((512, 512), lambda i: (0, i)),
        out_shape=jax.ShapeDtypeStruct((512, 1024), jnp.bfloat16),
        scratch_shapes=[pltpu.VMEM((2048, 128), jnp.float32)],
        name="last",
        compiler_params=pltpu.CompilerParams(vmem_limit_bytes=16 << 20),
    )(moved.reshape(4, 2, 2, 2, 2, 2, 32, 128))


def on_device(amplitudes, hop_blocks, coupling_seed):
    tables = prepare(hop_blocks, coupling_seed)
    sent, *tables = lax.optimization_barrier((step_one(amplitudes, hop_blocks), *tables))
    sent = exchange(sent, EX1)
    sent = exchange(step_two(sent, *tables), EX2)
    sent = exchange(step_three_four(sent, hop_blocks), EX3)
    return finish(sent)


def solution(mesh):
    fine = Mesh(mesh.devices.reshape(SIZES), AXES)
    spec = P(("z1", "z0", "yh", "y0"), ("zh", "core", "x"))
    return jax.shard_map(
        on_device, mesh=fine, in_specs=(spec, P(), P()), out_specs=spec, check_vma=False
    )
```

time: 134 us -> 122 us (0.910)
  blocking collectives: 58.5 us -> 112 us
  waiting for transfers between devices: 32.5 us -> 0 us
  starting transfers between devices: 21 us -> 0 us
  Pallas kernels: 20.8 us -> 7.1 us
  local copies, waits for them, and re-layouts: 0.97 us -> 2.45 us
    all_to_all x2 -> x3, blocking collectives: 58.5 us -> 112 us  [exchange(): return lax.all_to_all(value, axes, split_axis=0, concat_axis=0, tiled=True)]
    all_to_all x1 -> x0, waiting for transfers between devices: 32.5 us -> none  [exchange(): return lax.all_to_all(value, axes, split_axis=0, concat_axis=0, tiled=True)]
    all_to_all x1 -> x0, starting transfers between devices: 21 us -> none  [exchange(): return lax.all_to_all(value, axes, split_axis=0, concat_axis=0, tiled=True)]
    pallas_call x4, Pallas kernels: 18.2 us -> 5.82 us  [the longest x1 2.49 us: finish(): pl.pallas_call(last_kernel, grid=(2,), in_specs=[pl.BlockSpec((4, 2, 2, 2...]
    pallas_call x1, Pallas kernels: 2.62 us -> 1.28 us  [prepare(): pl.pallas_call(prepare_kernel, grid=(1,), in_specs=[smem, smem, pl.BlockS...]
  transfers between devices with their start and end apart: 1 -> 0, of which waited for: 1 -> 0; matrix products, arithmetic and copies ran while one was open for 0% -> 0% of each run, Pallas kernels for 2% -> 0%
where the time goes in v3:
time: 122 us
  blocking collectives  112 us (92%)
  Pallas kernels  7.1 us (6%)
  local copies, waits for them, and re-layouts  2.45 us (2%)
    all_to_all x3, blocking collectives, exchange(): return lax.all_to_all(value, axes, split_axis=0, concat_axis=0, tiled=True)  112 us
    pallas_call x1, Pallas kernels, finish(): pl.pallas_call(last_kernel, grid=(2,), in_specs=[pl.BlockSpec((4, 2, 2, 2...  2.49 us

profile of v3, /device:TPU:1, one launch (start us, length us, event | category | flops | bytes accessed | tf_op | source)
XLA Modules:
  0.0 121.8 jit_solution(10651286923822275099)
XLA Ops:
  0.0 0.0 copy-start
  0.0 0.0 copy-start.1
  0.0 1.2 %slice.3.hop_ref = bf16[1,512,512]{2,1,0:T(8,128)(2,1)S(1)} slice(bf16[4,512,512]{2,1,0:T(8,128)(2,1)} %high_ref.1), slice={[0:1], [0:512], [0:512]} | slice | bytes 1048576 | tf_op jit(solution)/shard_map/slice | solution.py:80
  1.3 0.0 copy-start.2
  1.3 1.2 copy-done.2
  2.5 1.0 first.1
  3.5 0.0 copy-done
  3.5 0.0 copy-done.1
  3.5 1.3 %prepare.1 = (bf16[512,512]{1,0:T(8,128)(2,1)S(1)}, f32[512,128]{1,0:T(8,128)S(1)}, f32[8,4,8,128]{3,2,1,0:T(8,128)S(1)}) custom-call(s32[14]{0:T(128)S(1)} %copy-done.1, s32[1]{0:T(128)} %bitcast.1.dev_ref, bf16[4,512,512]{2,1,0:T(8,128)(2,1)S(1)} %copy-done), custom_call_target="tpu_custom_call" | custom-call | flops 268435456 | bytes 1572864 | tf_op jit(solution)/shard_map/prepare/pallas_call | solution.py:126
  4.8 55.9 %all_to_all.15 = bf16[128,32,128]{2,1,0:T(8,128)(2,1)S(1)} all-to-all(bf16[128,32,128]{2,1,0:T(8,128)(2,1)S(1)} %bitcast.12), channel_id=1, replica_groups=mesh['zh'=2,'core'=2,'x'=4,'z1'=2,'z0'=2,'yh'=4,'y0'=2] {'zh','core','x'..., dimensions={0} | all-to-all | bytes 2097152 | tf_op jit(solution)/shard_map/all_to_all | solution.py:23
  60.7 0.7 second.1
  61.4 16.2 %all_to_all.16 = bf16[16,256,128]{2,1,0:T(8,128)(2,1)S(1)} all-to-all(bf16[16,256,128]{2,1,0:T(8,128)(2,1)S(1)} %bitcast.8), channel_id=1, replica_groups=mesh['zh'=2,'core'=2,'x'=4,'z1'=2,'z0'=2,'yh'=4,'y0'=2] {'x','z0','y0'}, dimensions={0} | all-to-all | bytes 2097152 | tf_op jit(solution)/shard_map/all_to_all | solution.py:23
  77.6 1.6 %third.1 = bf16[4,2,2,2,2,2,2,16,128]{8,7,6,5,4,3,2,1,0:T(8,128)(2,1)S(1)} custom-call(bf16[4,4,256,128]{3,2,1,0:T(8,128)(2,1)S(1)} %bitcast.10, bf16[4,512,512]{2,1,0:T(8,128)(2,1)S(1)} %copy-done, bf16[4,512,512]{2,1,0:T(8,128)(2,1)S(1)} %copy-done), custom_call_target="tpu_custom_call" | custom-call | flops 1073741824 | bytes 3145728 | tf_op jit(solution)/shard_map/third/pallas_call | solution.py:219
  79.2 40.1 %all_to_all.17 = bf16[128,32,128]{2,1,0:T(8,128)(2,1)S(1)} all-to-all(bf16[128,32,128]{2,1,0:T(8,128)(2,1)S(1)} %bitcast.11), channel_id=1, replica_groups=mesh['zh'=2,'core'=2,'x'=4,'z1'=2,'z0'=2,'yh'=4,'y0'=2] {'yh','y0','zh',..., dimensions={0} | all-to-all | bytes 2097152 | tf_op jit(solution)/shard_map/all_to_all | solution.py:23
  119.4 2.5 %last.1 = bf16[512,1024]{1,0:T(8,128)(2,1)} custom-call(bf16[4,2,2,2,2,2,32,128]{7,6,5,4,3,2,1,0:T(8,128)(2,1)S(1)} %bitcast.9), custom_call_target="tpu_custom_call" | custom-call | tf_op jit(solution)/shard_map/last/pallas_call | solution.py:265
Async XLA Ops:
  0.0 3.5 %copy-start = (bf16[4,512,512]{2,1,0:T(8,128)(2,1)S(1)}, bf16[4,512,512]{2,1,0:T(8,128)(2,1)}, u32[]{:S(2)}) copy-start(bf16[4,512,512]{2,1,0:T(8,128)(2,1)} %high_ref.1) | copy-start | bytes 6291460
  0.0 3.5 %copy-start.1 = (s32[14]{0:T(128)S(1)}, s32[14]{0:T(128)}, u32[]{:S(2)}) copy-start(s32[14]{0:T(128)} %seed_ref.1) | copy-start | bytes 172
  1.3 1.2 %copy-start.2 = (bf16[512,1024]{1,0:T(8,128)(2,1)S(1)}, bf16[512,1024]{1,0:T(8,128)(2,1)}, u32[]{:S(2)}) copy-start(bf16[512,1024]{1,0:T(8,128)(2,1)} %x_ref.1) | copy-start | bytes 3145732

commit v4 on v3

--- a/solution.py
+++ b/solution.py
@@ -11,7 +11,7 @@
 
 AXES = ("zh", "core", "x", "z1", "z0", "yh", "y0")
 SIZES = (2, 2, 4, 2, 2, 4, 2)
-EX1 = ("zh", "core", "x", "z1", "yh")
+EX1 = ("x", "yh", "zh", "z1", "core")
 EX2 = ("x", "z0", "y0")
 EX3 = ("yh", "y0", "zh", "z1", "z0", "core")
 
@@ -44,6 +44,10 @@
     return [choose([turned[(q - a) & 3] for q in range(4)]) for a in range(4)]
 
 
+def in_hbm(*arrays):
+    return [pltpu.with_memory_space_constraint(a, pltpu.HBM) for a in arrays]
+
+
 def permuted_rows(matrix, source):
     row = lax.broadcasted_iota(jnp.int32, (BLOCK, BLOCK), 0)
     col = lax.broadcasted_iota(jnp.int32, (BLOCK, BLOCK), 1)
@@ -51,47 +55,18 @@
     return product(pick, matrix, NN).astype(jnp.bfloat16)
 
 
-def first_kernel(x_ref, hop_ref, out_ref, rows_ref):
-    rows = permuted_rows(hop_ref[0], lambda r: ((r & 15) << 5) | (r >> 4))
-    for u9 in range(2):
-        first = product(rows, x_ref[:, u9 * 512 : (u9 + 1) * 512], NT).astype(jnp.bfloat16)
-        for x in range(4):
-            out_ref[:, x, :, u9 * 16 : (u9 + 1) * 16] = first[:, x * 128 : (x + 1) * 128].reshape(
-                4, 8, 16, 128
-            )
-
-
-def step_one(amplitudes, hop_blocks):
-    out = pl.pallas_call(
-        first_kernel,
-        grid=(1,),
-        in_specs=[
-            pl.BlockSpec((512, 1024), lambda i: (0, 0)),
-            pl.BlockSpec((1, 512, 512), lambda i: (0, 0, 0)),
-        ],
-        out_specs=pl.BlockSpec((4, 4, 8, 32, 128), lambda i: (0, 0, 0, 0, 0)),
-        out_shape=jax.ShapeDtypeStruct((4, 4, 8, 32, 128), jnp.bfloat16),
-        scratch_shapes=[pltpu.VMEM((8, 128), jnp.float32)],
-        cost_estimate=pl.CostEstimate(
-            flops=2 * 512 * 512 * 1536, bytes_accessed=5 << 19, transcendentals=0
-        ),
-        name="first",
-        compiler_params=pltpu.CompilerParams(vmem_limit_bytes=16 << 20),
-    )(amplitudes, hop_blocks[:1])
-    return out.reshape(128, 32, 128)
-
-
-def prepare_kernel(seed_ref, dev_ref, hop_ref, rows_ref, base_ref, side_ref):
-    def source(r):
-        return (
-            ((r & 4) << 6)
-            | ((r & 2) << 6)
-            | ((r >> 2) & 0x78)
-            | ((r & 1) << 2)
-            | ((r >> 3) & 3)
-        )
-
-    rows_ref[...] = permuted_rows(hop_ref[0], source)
+def first_kernel(
+    seed_ref, dev_ref, x_hbm, hop_hbm, out_ref, rows_ref, base_ref, side_ref, x_ref, hop_ref, sems
+):
+    copies = [
+        pltpu.make_async_copy(hop_hbm.at[0], hop_ref.at[0], sems.at[0]),
+        pltpu.make_async_copy(x_hbm.at[:, 0:512], x_ref.at[0], sems.at[1]),
+        pltpu.make_async_copy(x_hbm.at[:, 512:1024], x_ref.at[1], sems.at[2]),
+        pltpu.make_async_copy(hop_hbm.at[1], hop_ref.at[1], sems.at[3]),
+    ]
+    for copy in copies:
+        copy.start()
+
     cost = [COUPLING * seed_ref[i].astype(jnp.float32) for i in range(SITES)]
     place = dev_ref[0]
 
@@ -108,7 +83,7 @@
     energy = (cost[12] * z0) * bit(row, 1) + (cost[9] * y0) * bit(row, 6)
     energy += (cost[8] * x1) * bit(row, 5) + (cost[7] * x0) * bit(row, 0)
     energy += cost[6] * (bit(row, 4) * bit(lane, 6)) + cost[5] * (bit(row, 3) * bit(lane, 5))
-    for site, held in enumerate((y1, y2, z1, core, zh)):
+    for site, held in enumerate((core, z1, zh, y1, y2)):
         energy += (cost[site] * held) * bit(lane, site)
     base_ref[...] = jnp.exp(-energy)
     small = lax.broadcasted_iota(jnp.int32, (8, 128), 0)
@@ -119,37 +94,72 @@
             extra += cost[10] * float((g & 1) * (top & 1))
             side_ref[g, top] = jnp.exp(-extra)
 
-
-def prepare(hop_blocks, coupling_seed):
+    copies[0].wait()
+    rows = permuted_rows(hop_ref[0], lambda r: ((r & 15) << 5) | (r >> 4))
+    for u9 in range(2):
+        copies[1 + u9].wait()
+        first = product(rows, x_ref[u9], NT).astype(jnp.bfloat16)
+        for x in range(4):
+            out_ref[x, :, u9 * 16 : (u9 + 1) * 16] = first[:, x * 128 : (x + 1) * 128].reshape(
+                32, 16, 128
+            )
+
+    def source(r):
+        return (
+            ((r & 4) << 6)
+            | ((r & 2) << 6)
+            | ((r >> 2) & 0x78)
+            | ((r & 1) << 2)
+            | ((r >> 3) & 3)
+        )
+
+    copies[3].wait()
+    rows_ref[...] = permuted_rows(hop_ref[1], source)
+
+
+def step_one(amplitudes, hop_blocks, coupling_seed):
     place = lax.axis_index(AXES).astype(jnp.int32).reshape(1)
+    (coupling_seed,) = in_hbm(coupling_seed)
     smem = pl.BlockSpec(memory_space=pltpu.SMEM)
-    return pl.pallas_call(
-        prepare_kernel,
-        grid=(1,),
-        in_specs=[smem, smem, pl.BlockSpec((1, 512, 512), lambda i: (1, 0, 0))],
-        out_specs=[
-            pl.BlockSpec((512, 512), lambda i: (0, 0)),
-            pl.BlockSpec((512, 128), lambda i: (0, 0)),
-            pl.BlockSpec((8, 4, 8, 128), lambda i: (0, 0, 0, 0)),
-        ],
+    vmem = pl.BlockSpec(memory_space=pltpu.VMEM)
+    hbm = pl.BlockSpec(memory_space=pltpu.HBM)
+    out, rows, base, side = pl.pallas_call(
+        first_kernel,
+        in_specs=[smem, smem, hbm, hbm],
+        out_specs=[vmem, vmem, vmem, vmem],
         out_shape=[
+            jax.ShapeDtypeStruct((4, 32, 32, 128), jnp.bfloat16),
             jax.ShapeDtypeStruct((512, 512), jnp.bfloat16),
             jax.ShapeDtypeStruct((512, 128), jnp.float32),
             jax.ShapeDtypeStruct((8, 4, 8, 128), jnp.float32),
         ],
+        scratch_shapes=[
+            pltpu.VMEM((2, 512, 512), jnp.bfloat16),
+            pltpu.VMEM((2, 512, 512), jnp.bfloat16),
+            pltpu.SemaphoreType.DMA((4,)),
+        ],
         cost_estimate=pl.CostEstimate(
-            flops=2 * 512 * 512 * 512, bytes_accessed=3 << 19, transcendentals=1 << 17
+            flops=2 * 512 * 512 * 2048, bytes_accessed=5 << 19, transcendentals=1 << 17
         ),
-        name="prepare",
+        name="first",
         compiler_params=pltpu.CompilerParams(vmem_limit_bytes=16 << 20),
-    )(coupling_seed, place, hop_blocks)
+    )(coupling_seed, place, *in_hbm(amplitudes, hop_blocks))
+    return out.reshape(128, 32, 128), rows, base, side
+
+
+def gathered(moved_ref, g):
+    z1, yh = g >> 2, g & 3
+    return jnp.concatenate(
+        [moved_ref[x, yh, zh, z1, core] for zh in range(2) for core in range(2) for x in range(4)],
+        axis=0,
+    )
 
 
 def second_kernel(moved_ref, rows_ref, base_ref, side_ref, out_ref):
     base = base_ref[...].reshape(4, 16, 8, 128)
     for half in range(4):
         data = jnp.concatenate(
-            [moved_ref[:, half * 2 + g].reshape(512, 128) for g in range(2)], axis=1
+            [gathered(moved_ref, half * 2 + g) for g in range(2)], axis=1
         )
         second = product(rows_ref[...], data, NN)
         for b in range(2):
@@ -164,7 +174,7 @@
         second_kernel,
         grid=(1,),
         in_specs=[
-            pl.BlockSpec((16, 8, 32, 128), lambda i: (0, i, 0, 0)),
+            pl.BlockSpec((4, 4, 2, 2, 2, 32, 128), lambda i: (0, 0, 0, 0, 0, 0, 0)),
             pl.BlockSpec((512, 512), lambda i: (0, 0)),
             pl.BlockSpec((512, 128), lambda i: (0, 0)),
             pl.BlockSpec((8, 4, 8, 128), lambda i: (i, 0, 0, 0)),
@@ -176,7 +186,7 @@
         ),
         name="second",
         compiler_params=pltpu.CompilerParams(vmem_limit_bytes=16 << 20),
-    )(moved.reshape(16, 8, 32, 128), rows, base, side)
+    )(moved.reshape(4, 4, 2, 2, 2, 32, 128), rows, base, side)
     return out.reshape(16, 256, 128)
 
 
@@ -238,49 +248,57 @@
     return out.reshape(128, 32, 128)
 
 
-def last_kernel(moved_ref, out_ref, held_ref):
+def last_kernel(moved_ref, out_hbm, held_ref, out_ref, sems):
     row = lax.broadcasted_iota(jnp.int32, (128, 128), 0)
     col = lax.broadcasted_iota(jnp.int32, (128, 128), 1)
     eye = jnp.where(row == col, 1.0, 0.0).astype(jnp.bfloat16)
-    for pair in range(2):
+    copies = []
+    for pair in range(4):
         u9, u8 = pair >> 1, pair & 1
         for low in range(32):
-            u4, u3, u2, u10 = low >> 4, (low >> 3) & 1, (low >> 2) & 1, low & 3
-            block = moved_ref[u10, u8, u4, u2, u9, u3].astype(jnp.float32)
+            block = moved_ref[low >> 3, u8, (low >> 2) & 1, (low >> 1) & 1, u9, low & 1]
             for u7 in range(2):
                 at = ((pair * 2 + u7) * 32 + low) * 16
-                held_ref[at : at + 16, :] = block[u7 * 16 : u7 * 16 + 16]
-    for lane in range(4):
-        for top in range(4):
-            parts = [
-                held_ref[pl.ds(lane * 512 + top * 4 + j, 32, stride=16), :] for j in range(4)
-            ]
-            tile = jnp.concatenate(swap_groups(parts), axis=0).astype(jnp.bfloat16)
-            out_ref[top * 128 : (top + 1) * 128, lane * 128 : (lane + 1) * 128] = product(
-                eye, tile, NT
-            ).astype(jnp.bfloat16)
+                held_ref[at : at + 16, :] = block[u7 * 16 : u7 * 16 + 16].astype(jnp.float32)
+        for u7 in range(2):
+            for top in range(4):
+                parts = [
+                    held_ref[pl.ds((pair * 2 + u7) * 512 + top * 4 + j, 32, stride=16), :]
+                    for j in range(4)
+                ]
+                tile = jnp.concatenate(swap_groups(parts), axis=0).astype(jnp.bfloat16)
+                out_ref[pair, top * 128 : (top + 1) * 128, u7 * 128 : (u7 + 1) * 128] = product(
+                    eye, tile, NT
+                ).astype(jnp.bfloat16)
+        copy = pltpu.make_async_copy(
+            out_ref.at[pair], out_hbm.at[:, pair * 256 : (pair + 1) * 256], sems.at[pair]
+        )
+        copy.start()
+        copies.append(copy)
+    for copy in copies:
+        copy.wait()
 
 
 def finish(moved):
     return pl.pallas_call(
         last_kernel,
-        grid=(2,),
-        in_specs=[
-            pl.BlockSpec((4, 2, 2, 2, 1, 2, 32, 128), lambda i: (0, 0, 0, 0, i, 0, 0, 0))
-        ],
-        out_specs=pl.BlockSpec((512, 512), lambda i: (0, i)),
+        in_specs=[pl.BlockSpec(memory_space=pltpu.VMEM)],
+        out_specs=pl.BlockSpec(memory_space=pltpu.HBM),
         out_shape=jax.ShapeDtypeStruct((512, 1024), jnp.bfloat16),
-        scratch_shapes=[pltpu.VMEM((2048, 128), jnp.float32)],
+        scratch_shapes=[
+            pltpu.VMEM((4096, 128), jnp.float32),
+            pltpu.VMEM((4, 512, 256), jnp.bfloat16),
+            pltpu.SemaphoreType.DMA((4,)),
+        ],
         name="last",
         compiler_params=pltpu.CompilerParams(vmem_limit_bytes=16 << 20),
     )(moved.reshape(4, 2, 2, 2, 2, 2, 32, 128))
 
 
 def on_device(amplitudes, hop_blocks, coupling_seed):
-    tables = prepare(hop_blocks, coupling_seed)
-    sent, *tables = lax.optimization_barrier((step_one(amplitudes, hop_blocks), *tables))
+    sent, rows, base, side = step_one(amplitudes, hop_blocks, coupling_seed)
     sent = exchange(sent, EX1)
-    sent = exchange(step_two(sent, *tables), EX2)
+    sent = exchange(step_two(sent, rows, base, side), EX2)
     sent = exchange(step_three_four(sent, hop_blocks), EX3)
     return finish(sent)
 

time: 122 us -> 121 us (level)
  local copies, waits for them, and re-layouts: 2.45 us -> 0.01 us
    slice x1 -> x0, local copies, waits for them, and re-layouts: 1.22 us -> none  [step_one(): hop_blocks[:1]]
    unnamed x6 -> x2, local copies, waits for them, and re-layouts: 1.23 us -> 0.01 us
    pallas_call x4 -> x3, Pallas kernels: 5.47 us -> 6.57 us  [the longest x1 3.58 us: step_one(): pl.pallas_call(first_kernel, in_specs=[smem, smem, hbm, hbm], out_specs=[...]
where the time goes in v4:
time: 121 us; the launch traced here: 120 us
  blocking collectives  112 us (93%)
  Pallas kernels  8.2 us (7%)
    all_to_all x3, blocking collectives, exchange(): return lax.all_to_all(value, axes, split_axis=0, concat_axis=0, tiled=True)  112 us
    pallas_call x1, Pallas kernels, step_one(): pl.pallas_call(first_kernel, in_specs=[smem, smem, hbm, hbm], out_specs=[...  3.58 us

profile of v4, /device:TPU:1, one launch (start us, length us, event | category | flops | bytes accessed | tf_op | source)
XLA Modules:
  0.0 120.4 jit_solution(15686216442954444026)
XLA Ops:
  0.0 3.6 %first.1 = (bf16[4,32,32,128]{3,2,1,0:T(8,128)(2,1)S(1)}, bf16[512,512]{1,0:T(8,128)(2,1)S(1)}, f32[512,128]{1,0:T(8,128)S(1)}, f32[8,4,8,128]{3,2,1,0:T(8,128)S(1)}) custom-call(s32[14]{0:T(128)} %seed_ref.1, s32[1]{0:T(128)} %bitcast.dev_ref, bf16[512,1024]{1,0:T(8,128)(2,1)} %x_hbm.1, bf16[4,512,512]{2,1,0:T(8,128)(2,1)} %high_ref.1), custom_call_target="tpu_custom_call" | custom-call | flops 1073741824 | bytes 2621440 | tf_op jit(solution)/shard_map/first/pallas_call | solution.py:126
  3.6 55.7 %all_to_all.15 = bf16[128,32,128]{2,1,0:T(8,128)(2,1)S(1)} all-to-all(bf16[128,32,128]{2,1,0:T(8,128)(2,1)S(1)} %bitcast.12), channel_id=1, replica_groups=mesh['zh'=2,'core'=2,'x'=4,'z1'=2,'z0'=2,'yh'=4,'y0'=2] {'x','yh','zh','..., dimensions={0} | all-to-all | bytes 2097152 | tf_op jit(solution)/shard_map/all_to_all | solution.py:23
  59.3 0.0 copy-start
  59.3 0.7 second.1
  60.1 15.6 %all_to_all.16 = bf16[16,256,128]{2,1,0:T(8,128)(2,1)S(1)} all-to-all(bf16[16,256,128]{2,1,0:T(8,128)(2,1)S(1)} %bitcast.8), channel_id=1, replica_groups=mesh['zh'=2,'core'=2,'x'=4,'z1'=2,'z0'=2,'yh'=4,'y0'=2] {'x','z0','y0'}, dimensions={0} | all-to-all | bytes 2097152 | tf_op jit(solution)/shard_map/all_to_all | solution.py:23
  75.7 0.0 copy-done
  75.7 1.6 %third.1 = bf16[4,2,2,2,2,2,2,16,128]{8,7,6,5,4,3,2,1,0:T(8,128)(2,1)S(1)} custom-call(bf16[4,4,256,128]{3,2,1,0:T(8,128)(2,1)S(1)} %bitcast.10, bf16[4,512,512]{2,1,0:T(8,128)(2,1)S(1)} %copy-done, bf16[4,512,512]{2,1,0:T(8,128)(2,1)S(1)} %copy-done), custom_call_target="tpu_custom_call" | custom-call | flops 1073741824 | bytes 3145728 | tf_op jit(solution)/shard_map/third/pallas_call | solution.py:229
  77.3 40.8 %all_to_all.17 = bf16[128,32,128]{2,1,0:T(8,128)(2,1)S(1)} all-to-all(bf16[128,32,128]{2,1,0:T(8,128)(2,1)S(1)} %bitcast.11), channel_id=1, replica_groups=mesh['zh'=2,'core'=2,'x'=4,'z1'=2,'z0'=2,'yh'=4,'y0'=2] {'yh','y0','zh',..., dimensions={0} | all-to-all | bytes 2097152 | tf_op jit(solution)/shard_map/all_to_all | solution.py:23
  118.1 2.3 %last.1 = bf16[512,1024]{1,0:T(8,128)(2,1)} custom-call(bf16[4,2,2,2,2,2,32,128]{7,6,5,4,3,2,1,0:T(8,128)(2,1)S(1)} %bitcast.9), custom_call_target="tpu_custom_call" | custom-call | tf_op jit(solution)/shard_map/last/pallas_call | solution.py:283
Async XLA Ops:
  59.3 16.4 %copy-start = (bf16[4,512,512]{2,1,0:T(8,128)(2,1)S(1)}, bf16[4,512,512]{2,1,0:T(8,128)(2,1)}, u32[]{:S(2)}) copy-start(bf16[4,512,512]{2,1,0:T(8,128)(2,1)} %high_ref.1) | copy-start | bytes 6291460

commit v5 on v4

--- a/solution.py
+++ b/solution.py
@@ -19,8 +19,34 @@
 NN = (((1,), (0,)), ((), ()))
 
 
-def exchange(value, axes):
-    return lax.all_to_all(value, axes, split_axis=0, concat_axis=0, tiled=True)
+def order_one():
+    members = []
+    for r in range(128):
+        a, b, c, core = (r >> 1) & 3, (r >> 3) & 3, r >> 5, r & 1
+        x, y, z = a, (b - a) & 3, (c + a) & 3
+        members.append((((x * 4 + y) * 4 + z) << 1) | core)
+    return members
+
+
+def order_three():
+    members = []
+    for r in range(128):
+        a, b, core = (r >> 1) & 7, r >> 4, r & 1
+        y, z = (b + 3 * a) & 7, (3 * a) & 7
+        members.append(((y * 8 + z) << 1) | core)
+    return members
+
+
+MEMBERS1, MEMBERS3 = order_one(), order_three()
+SLOT1 = [MEMBERS1.index(m) for m in range(128)]
+SLOT3 = [MEMBERS3.index(m) for m in range(128)]
+
+
+def exchange(value, axes, members=None):
+    groups = None if members is None else [members]
+    return lax.all_to_all(
+        value, axes, split_axis=0, concat_axis=0, tiled=True, axis_index_groups=groups
+    )
 
 
 def product(left, right, dims):
@@ -100,9 +126,10 @@
         copies[1 + u9].wait()
         first = product(rows, x_ref[u9], NT).astype(jnp.bfloat16)
         for x in range(4):
-            out_ref[x, :, u9 * 16 : (u9 + 1) * 16] = first[:, x * 128 : (x + 1) * 128].reshape(
-                32, 16, 128
-            )
+            for low in range(32):
+                out_ref[SLOT1[x * 32 + low], u9 * 16 : (u9 + 1) * 16] = first[
+                    low * 16 : low * 16 + 16, x * 128 : (x + 1) * 128
+                ]
 
     def source(r):
         return (
@@ -128,7 +155,7 @@
         in_specs=[smem, smem, hbm, hbm],
         out_specs=[vmem, vmem, vmem, vmem],
         out_shape=[
-            jax.ShapeDtypeStruct((4, 32, 32, 128), jnp.bfloat16),
+            jax.ShapeDtypeStruct((128, 32, 128), jnp.bfloat16),
             jax.ShapeDtypeStruct((512, 512), jnp.bfloat16),
             jax.ShapeDtypeStruct((512, 128), jnp.float32),
             jax.ShapeDtypeStruct((8, 4, 8, 128), jnp.float32),
@@ -144,13 +171,18 @@
         name="first",
         compiler_params=pltpu.CompilerParams(vmem_limit_bytes=16 << 20),
     )(coupling_seed, place, *in_hbm(amplitudes, hop_blocks))
-    return out.reshape(128, 32, 128), rows, base, side
+    return out, rows, base, side
 
 
 def gathered(moved_ref, g):
     z1, yh = g >> 2, g & 3
     return jnp.concatenate(
-        [moved_ref[x, yh, zh, z1, core] for zh in range(2) for core in range(2) for x in range(4)],
+        [
+            moved_ref[SLOT1[x * 32 + yh * 8 + zh * 4 + z1 * 2 + core]]
+            for zh in range(2)
+            for core in range(2)
+            for x in range(4)
+        ],
         axis=0,
     )
 
@@ -174,7 +206,7 @@
         second_kernel,
         grid=(1,),
         in_specs=[
-            pl.BlockSpec((4, 4, 2, 2, 2, 32, 128), lambda i: (0, 0, 0, 0, 0, 0, 0)),
+            pl.BlockSpec((128, 32, 128), lambda i: (0, 0, 0)),
             pl.BlockSpec((512, 512), lambda i: (0, 0)),
             pl.BlockSpec((512, 128), lambda i: (0, 0)),
             pl.BlockSpec((8, 4, 8, 128), lambda i: (i, 0, 0, 0)),
@@ -186,7 +218,7 @@
         ),
         name="second",
         compiler_params=pltpu.CompilerParams(vmem_limit_bytes=16 << 20),
-    )(moved.reshape(4, 4, 2, 2, 2, 32, 128), rows, base, side)
+    )(moved, rows, base, side)
     return out.reshape(16, 256, 128)
 
 
@@ -220,7 +252,8 @@
         for b in range(2):
             for r in range(32):
                 d13, d12, mid, d9 = r >> 4, (r >> 3) & 1, (r >> 1) & 3, r & 1
-                out_ref[mid, d9, step >> 1, d13, d12, step & 1, b] = fourth[
+                member = mid * 32 + d9 * 16 + (step >> 1) * 8 + d13 * 4 + d12 * 2 + (step & 1)
+                out_ref[SLOT3[member], b * 16 : b * 16 + 16] = fourth[
                     r * 16 : r * 16 + 16, b * 128 : (b + 1) * 128
                 ]
 
@@ -234,10 +267,8 @@
             pl.BlockSpec((1, 512, 512), lambda i: (2, 0, 0)),
             pl.BlockSpec((1, 512, 512), lambda i: (3, 0, 0)),
         ],
-        out_specs=pl.BlockSpec(
-            (4, 2, 2, 2, 2, 2, 2, 16, 128), lambda i: (0, 0, 0, 0, 0, 0, 0, 0, 0)
-        ),
-        out_shape=jax.ShapeDtypeStruct((4, 2, 2, 2, 2, 2, 2, 16, 128), jnp.bfloat16),
+        out_specs=pl.BlockSpec((128, 32, 128), lambda i: (0, 0, 0)),
+        out_shape=jax.ShapeDtypeStruct((128, 32, 128), jnp.bfloat16),
         scratch_shapes=[pltpu.VMEM((4096, 128), jnp.float32)],
         cost_estimate=pl.CostEstimate(
             flops=4 * 512 * 512 * 1024, bytes_accessed=3 << 20, transcendentals=0
@@ -245,7 +276,7 @@
         name="third",
         compiler_params=pltpu.CompilerParams(vmem_limit_bytes=16 << 20),
     )(moved.reshape(4, 4, 256, 128), hop_blocks, hop_blocks)
-    return out.reshape(128, 32, 128)
+    return out
 
 
 def last_kernel(moved_ref, out_hbm, held_ref, out_ref, sems):
@@ -256,7 +287,8 @@
     for pair in range(4):
         u9, u8 = pair >> 1, pair & 1
         for low in range(32):
-            block = moved_ref[low >> 3, u8, (low >> 2) & 1, (low >> 1) & 1, u9, low & 1]
+            member = (low >> 3) * 32 + u8 * 16 + ((low >> 1) & 3) * 4 + u9 * 2 + (low & 1)
+            block = moved_ref[SLOT3[member]]
             for u7 in range(2):
                 at = ((pair * 2 + u7) * 32 + low) * 16
                 held_ref[at : at + 16, :] = block[u7 * 16 : u7 * 16 + 16].astype(jnp.float32)
@@ -292,14 +324,14 @@
         ],
         name="last",
         compiler_params=pltpu.CompilerParams(vmem_limit_bytes=16 << 20),
-    )(moved.reshape(4, 2, 2, 2, 2, 2, 32, 128))
+    )(moved)
 
 
 def on_device(amplitudes, hop_blocks, coupling_seed):
     sent, rows, base, side = step_one(amplitudes, hop_blocks, coupling_seed)
-    sent = exchange(sent, EX1)
+    sent = exchange(sent, EX1, MEMBERS1)
     sent = exchange(step_two(sent, rows, base, side), EX2)
-    sent = exchange(step_three_four(sent, hop_blocks), EX3)
+    sent = exchange(step_three_four(sent, hop_blocks), EX3, MEMBERS3)
     return finish(sent)
 
 

time: 121 us -> 124 us (1.025)
  blocking collectives: 112 us -> 115 us
    all_to_all x3, blocking collectives: 112 us -> 115 us  [exchange(): lax.all_to_all(value, axes, split_axis=0, concat_axis=0, tiled=True, axis...]
where the time goes in v5:
time: 124 us
  blocking collectives  115 us (93%)
  Pallas kernels  8.19 us (7%)
    all_to_all x3, blocking collectives, exchange(): lax.all_to_all(value, axes, split_axis=0, concat_axis=0, tiled=True, axis...  115 us
    pallas_call x1, Pallas kernels, step_one(): pl.pallas_call(first_kernel, in_specs=[smem, smem, hbm, hbm], out_specs=[...  3.58 us

profile of v5, /device:TPU:1, one launch (start us, length us, event | category | flops | bytes accessed | tf_op | source)
XLA Modules:
  0.0 123.6 jit_solution(5098124089884308022)
XLA Ops:
  0.0 3.6 %first.1 = (bf16[128,32,128]{2,1,0:T(8,128)(2,1)S(1)}, bf16[512,512]{1,0:T(8,128)(2,1)S(1)}, f32[512,128]{1,0:T(8,128)S(1)}, f32[8,4,8,128]{3,2,1,0:T(8,128)S(1)}) custom-call(s32[14]{0:T(128)} %seed_ref.1, s32[1]{0:T(128)} %bitcast.dev_ref, bf16[512,1024]{1,0:T(8,128)(2,1)} %x_hbm.1, bf16[4,512,512]{2,1,0:T(8,128)(2,1)} %high_ref.1), custom_call_target="tpu_custom_call" | custom-call | flops 1073741824 | bytes 2621440 | tf_op jit(solution)/shard_map/first/pallas_call | solution.py:153
  3.6 54.6 %all_to_all.15.moved_ref = bf16[128,32,128]{2,1,0:T(8,128)(2,1)S(1)} all-to-all(bf16[128,32,128]{2,1,0:T(8,128)(2,1)S(1)} %get-tuple-element.9), channel_id=1, replica_groups={{0,128,54,182,324,452,370,498,2,130,48,176,326,454,372,500,4,132,50,178..., dimensions={0} | all-to-all | bytes 2097152 | tf_op jit(solution)/shard_map/all_to_all | solution.py:47
  58.2 0.0 copy-start
  58.2 0.7 second.1
  58.9 17.3 %all_to_all.16 = bf16[16,256,128]{2,1,0:T(8,128)(2,1)S(1)} all-to-all(bf16[16,256,128]{2,1,0:T(8,128)(2,1)S(1)} %bitcast.3), channel_id=1, replica_groups=mesh['zh'=2,'core'=2,'x'=4,'z1'=2,'z0'=2,'yh'=4,'y0'=2] {'x','z0','y0'}, dimensions={0} | all-to-all | bytes 2097152 | tf_op jit(solution)/shard_map/all_to_all | solution.py:47
  76.2 0.0 copy-done
  76.2 1.6 %third.1 = bf16[128,32,128]{2,1,0:T(8,128)(2,1)S(1)} custom-call(bf16[4,4,256,128]{3,2,1,0:T(8,128)(2,1)S(1)} %bitcast.4, bf16[4,512,512]{2,1,0:T(8,128)(2,1)S(1)} %copy-done, bf16[4,512,512]{2,1,0:T(8,128)(2,1)S(1)} %copy-done), custom_call_target="tpu_custom_call" | custom-call | flops 1073741824 | bytes 3145728 | tf_op jit(solution)/shard_map/third/pallas_call | solution.py:262
  77.8 43.5 %all_to_all.17.moved_ref = bf16[128,32,128]{2,1,0:T(8,128)(2,1)S(1)} all-to-all(bf16[128,32,128]{2,1,0:T(8,128)(2,1)S(1)} %third.1), channel_id=1, replica_groups={{0,128,27,155,278,406,9,137,260,388,287,415,18,146,269,397,1,129,28,156..., dimensions={0} | all-to-all | bytes 2097152 | tf_op jit(solution)/shard_map/all_to_all | solution.py:47
  121.3 2.3 %last.1 = bf16[512,1024]{1,0:T(8,128)(2,1)} custom-call(bf16[128,32,128]{2,1,0:T(8,128)(2,1)S(1)} %all_to_all.17.moved_ref), custom_call_target="tpu_custom_call" | custom-call | tf_op jit(solution)/shard_map/last/pallas_call | solution.py:315
Async XLA Ops:
  58.2 18.0 %copy-start = (bf16[4,512,512]{2,1,0:T(8,128)(2,1)S(1)}, bf16[4,512,512]{2,1,0:T(8,128)(2,1)}, u32[]{:S(2)}) copy-start(bf16[4,512,512]{2,1,0:T(8,128)(2,1)} %high_ref.1) | copy-start | bytes 6291460

commit v6 on v5

--- a/solution.py
+++ b/solution.py
@@ -13,40 +13,17 @@
 SIZES = (2, 2, 4, 2, 2, 4, 2)
 EX1 = ("x", "yh", "zh", "z1", "core")
 EX2 = ("x", "z0", "y0")
-EX3 = ("yh", "y0", "zh", "z1", "z0", "core")
+EX3 = ("core", "yh", "y0", "zh", "z1", "z0")
 
 NT = (((1,), (1,)), ((), ()))
 NN = (((1,), (0,)), ((), ()))
 
 
-def order_one():
-    members = []
-    for r in range(128):
-        a, b, c, core = (r >> 1) & 3, (r >> 3) & 3, r >> 5, r & 1
-        x, y, z = a, (b - a) & 3, (c + a) & 3
-        members.append((((x * 4 + y) * 4 + z) << 1) | core)
-    return members
-
-
-def order_three():
-    members = []
-    for r in range(128):
-        a, b, core = (r >> 1) & 7, r >> 4, r & 1
-        y, z = (b + 3 * a) & 7, (3 * a) & 7
-        members.append(((y * 8 + z) << 1) | core)
-    return members
-
-
-MEMBERS1, MEMBERS3 = order_one(), order_three()
-SLOT1 = [MEMBERS1.index(m) for m in range(128)]
-SLOT3 = [MEMBERS3.index(m) for m in range(128)]
-
-
-def exchange(value, axes, members=None):
-    groups = None if members is None else [members]
-    return lax.all_to_all(
-        value, axes, split_axis=0, concat_axis=0, tiled=True, axis_index_groups=groups
-    )
+SLOT3 = [(m & 1) * 64 + (m >> 1) for m in range(128)]
+
+
+def exchange(value, axes):
+    return lax.all_to_all(value, axes, split_axis=0, concat_axis=0, tiled=True)
 
 
 def product(left, right, dims):
@@ -74,10 +51,13 @@
     return [pltpu.with_memory_space_constraint(a, pltpu.HBM) for a in arrays]
 
 
-def permuted_rows(matrix, source):
-    row = lax.broadcasted_iota(jnp.int32, (BLOCK, BLOCK), 0)
-    col = lax.broadcasted_iota(jnp.int32, (BLOCK, BLOCK), 1)
-    pick = jnp.where(col == source(row), 1.0, 0.0).astype(jnp.bfloat16)
+def permuted_rows(matrix, inner, outer):
+    row = lax.broadcasted_iota(jnp.int32, (16, BLOCK), 0)
+    col = lax.broadcasted_iota(jnp.int32, (16, BLOCK), 1)
+    apart = col - inner(row)
+    pick = jnp.concatenate(
+        [jnp.where(apart == outer(t), 1.0, 0.0).astype(jnp.bfloat16) for t in range(32)], axis=0
+    )
     return product(pick, matrix, NN).astype(jnp.bfloat16)
 
 
@@ -100,8 +80,8 @@
         return ((place >> shift) & 1).astype(jnp.float32)
 
     zh, core, x1, x0, z1, z0, y2, y1, y0 = [at(8 - b) for b in range(9)]
-    row = lax.broadcasted_iota(jnp.int32, (BLOCK, 128), 0)
-    lane = lax.broadcasted_iota(jnp.int32, (BLOCK, 128), 1)
+    row = lax.broadcasted_iota(jnp.int32, (128, 128), 0)
+    lane = lax.broadcasted_iota(jnp.int32, (128, 128), 1)
 
     def bit(index, shift):
         return ((index >> shift) & 1).astype(jnp.float32)
@@ -121,27 +101,22 @@
             side_ref[g, top] = jnp.exp(-extra)
 
     copies[0].wait()
-    rows = permuted_rows(hop_ref[0], lambda r: ((r & 15) << 5) | (r >> 4))
+    rows = permuted_rows(hop_ref[0], lambda s: s << 5, lambda t: t)
     for u9 in range(2):
         copies[1 + u9].wait()
         first = product(rows, x_ref[u9], NT).astype(jnp.bfloat16)
         for x in range(4):
             for low in range(32):
-                out_ref[SLOT1[x * 32 + low], u9 * 16 : (u9 + 1) * 16] = first[
+                out_ref[x * 32 + low, u9 * 16 : (u9 + 1) * 16] = first[
                     low * 16 : low * 16 + 16, x * 128 : (x + 1) * 128
                 ]
 
-    def source(r):
-        return (
-            ((r & 4) << 6)
-            | ((r & 2) << 6)
-            | ((r >> 2) & 0x78)
-            | ((r & 1) << 2)
-            | ((r >> 3) & 3)
-        )
-
     copies[3].wait()
-    rows_ref[...] = permuted_rows(hop_ref[1], source)
+    rows_ref[...] = permuted_rows(
+        hop_ref[1],
+        lambda s: ((s & 6) << 6) + ((s & 1) << 2) + (s >> 3),
+        lambda t: ((t >> 1) << 3) + ((t & 1) << 1),
+    )
 
 
 def step_one(amplitudes, hop_blocks, coupling_seed):
@@ -157,7 +132,7 @@
         out_shape=[
             jax.ShapeDtypeStruct((128, 32, 128), jnp.bfloat16),
             jax.ShapeDtypeStruct((512, 512), jnp.bfloat16),
-            jax.ShapeDtypeStruct((512, 128), jnp.float32),
+            jax.ShapeDtypeStruct((128, 128), jnp.float32),
             jax.ShapeDtypeStruct((8, 4, 8, 128), jnp.float32),
         ],
         scratch_shapes=[
@@ -178,7 +153,7 @@
     z1, yh = g >> 2, g & 3
     return jnp.concatenate(
         [
-            moved_ref[SLOT1[x * 32 + yh * 8 + zh * 4 + z1 * 2 + core]]
+            moved_ref[x * 32 + yh * 8 + zh * 4 + z1 * 2 + core]
             for zh in range(2)
             for core in range(2)
             for x in range(4)
@@ -188,7 +163,7 @@
 
 
 def second_kernel(moved_ref, rows_ref, base_ref, side_ref, out_ref):
-    base = base_ref[...].reshape(4, 16, 8, 128)
+    base = base_ref[...].reshape(1, 16, 8, 128)
     for half in range(4):
         data = jnp.concatenate(
             [gathered(moved_ref, half * 2 + g) for g in range(2)], axis=1
@@ -208,7 +183,7 @@
         in_specs=[
             pl.BlockSpec((128, 32, 128), lambda i: (0, 0, 0)),
             pl.BlockSpec((512, 512), lambda i: (0, 0)),
-            pl.BlockSpec((512, 128), lambda i: (0, 0)),
+            pl.BlockSpec((128, 128), lambda i: (0, 0)),
             pl.BlockSpec((8, 4, 8, 128), lambda i: (i, 0, 0, 0)),
         ],
         out_specs=pl.BlockSpec((16, 8, 32, 128), lambda i: (0, i, 0, 0)),
@@ -329,9 +304,9 @@
 
 def on_device(amplitudes, hop_blocks, coupling_seed):
     sent, rows, base, side = step_one(amplitudes, hop_blocks, coupling_seed)
-    sent = exchange(sent, EX1, MEMBERS1)
+    sent = exchange(sent, EX1)
     sent = exchange(step_two(sent, rows, base, side), EX2)
-    sent = exchange(step_three_four(sent, hop_blocks), EX3, MEMBERS3)
+    sent = exchange(step_three_four(sent, hop_blocks), EX3)
     return finish(sent)
 
 

time: 124 us -> 122 us (0.984)
  blocking collectives: 115 us -> 113 us
    all_to_all x3, blocking collectives: 115 us -> 113 us  [exchange(): return lax.all_to_all(value, axes, split_axis=0, concat_axis=0, tiled=True)]
where the time goes in v6:
time: 122 us
  blocking collectives  113 us (93%)
  Pallas kernels  8.22 us (7%)
    all_to_all x3, blocking collectives, exchange(): return lax.all_to_all(value, axes, split_axis=0, concat_axis=0, tiled=True)  113 us
    pallas_call x1, Pallas kernels, step_one(): pl.pallas_call(first_kernel, in_specs=[smem, smem, hbm, hbm], out_specs=[...  3.56 us

profile of v6, /device:TPU:1, one launch (start us, length us, event | category | flops | bytes accessed | tf_op | source)
XLA Modules:
  0.0 121.7 jit_solution(14177008466282162648)
XLA Ops:
  0.0 3.6 %first.1 = (bf16[128,32,128]{2,1,0:T(8,128)(2,1)S(1)}, bf16[512,512]{1,0:T(8,128)(2,1)S(1)}, f32[128,128]{1,0:T(8,128)S(1)}, f32[8,4,8,128]{3,2,1,0:T(8,128)S(1)}) custom-call(s32[14]{0:T(128)} %seed_ref.1, s32[1]{0:T(128)} %bitcast.dev_ref, bf16[512,1024]{1,0:T(8,128)(2,1)} %x_hbm.1, bf16[4,512,512]{2,1,0:T(8,128)(2,1)} %high_ref.1), custom_call_target="tpu_custom_call" | custom-call | flops 1073741824 | bytes 2621440 | tf_op jit(solution)/shard_map/first/pallas_call | solution.py:128
  3.6 55.8 %all_to_all.15.moved_ref = bf16[128,32,128]{2,1,0:T(8,128)(2,1)S(1)} all-to-all(bf16[128,32,128]{2,1,0:T(8,128)(2,1)S(1)} %get-tuple-element.9), channel_id=1, replica_groups=mesh['zh'=2,'core'=2,'x'=4,'z1'=2,'z0'=2,'yh'=4,'y0'=2] {'x','yh','zh','..., dimensions={0} | all-to-all | bytes 2097152 | tf_op jit(solution)/shard_map/all_to_all | solution.py:26
  59.3 0.0 copy-start
  59.3 0.7 second.1
  60.1 15.6 %all_to_all.16 = bf16[16,256,128]{2,1,0:T(8,128)(2,1)S(1)} all-to-all(bf16[16,256,128]{2,1,0:T(8,128)(2,1)S(1)} %bitcast.3), channel_id=1, replica_groups=mesh['zh'=2,'core'=2,'x'=4,'z1'=2,'z0'=2,'yh'=4,'y0'=2] {'x','z0','y0'}, dimensions={0} | all-to-all | bytes 2097152 | tf_op jit(solution)/shard_map/all_to_all | solution.py:26
  75.7 0.0 copy-done
  75.7 1.6 %third.1 = bf16[128,32,128]{2,1,0:T(8,128)(2,1)S(1)} custom-call(bf16[4,4,256,128]{3,2,1,0:T(8,128)(2,1)S(1)} %bitcast.4, bf16[4,512,512]{2,1,0:T(8,128)(2,1)S(1)} %copy-done, bf16[4,512,512]{2,1,0:T(8,128)(2,1)S(1)} %copy-done), custom_call_target="tpu_custom_call" | custom-call | flops 1073741824 | bytes 3145728 | tf_op jit(solution)/shard_map/third/pallas_call | solution.py:237
  77.3 42.1 %all_to_all.17.moved_ref = bf16[128,32,128]{2,1,0:T(8,128)(2,1)S(1)} all-to-all(bf16[128,32,128]{2,1,0:T(8,128)(2,1)S(1)} %third.1), channel_id=1, replica_groups=mesh['zh'=2,'core'=2,'x'=4,'z1'=2,'z0'=2,'yh'=4,'y0'=2] {'core','yh','y0..., dimensions={0} | all-to-all | bytes 2097152 | tf_op jit(solution)/shard_map/all_to_all | solution.py:26
  119.4 2.3 %last.1 = bf16[512,1024]{1,0:T(8,128)(2,1)} custom-call(bf16[128,32,128]{2,1,0:T(8,128)(2,1)S(1)} %all_to_all.17.moved_ref), custom_call_target="tpu_custom_call" | custom-call | tf_op jit(solution)/shard_map/last/pallas_call | solution.py:290
Async XLA Ops:
  59.3 16.3 %copy-start = (bf16[4,512,512]{2,1,0:T(8,128)(2,1)S(1)}, bf16[4,512,512]{2,1,0:T(8,128)(2,1)}, u32[]{:S(2)}) copy-start(bf16[4,512,512]{2,1,0:T(8,128)(2,1)} %high_ref.1) | copy-start | bytes 6291460

commit v7 on v6

--- a/solution.py
+++ b/solution.py
@@ -13,13 +13,10 @@
 SIZES = (2, 2, 4, 2, 2, 4, 2)
 EX1 = ("x", "yh", "zh", "z1", "core")
 EX2 = ("x", "z0", "y0")
-EX3 = ("core", "yh", "y0", "zh", "z1", "z0")
+EX3 = ("yh", "y0", "zh", "z1", "z0", "core")
 
 NT = (((1,), (1,)), ((), ()))
 NN = (((1,), (0,)), ((), ()))
-
-
-SLOT3 = [(m & 1) * 64 + (m >> 1) for m in range(128)]
 
 
 def exchange(value, axes):
@@ -228,7 +225,7 @@
             for r in range(32):
                 d13, d12, mid, d9 = r >> 4, (r >> 3) & 1, (r >> 1) & 3, r & 1
                 member = mid * 32 + d9 * 16 + (step >> 1) * 8 + d13 * 4 + d12 * 2 + (step & 1)
-                out_ref[SLOT3[member], b * 16 : b * 16 + 16] = fourth[
+                out_ref[member, b * 16 : b * 16 + 16] = fourth[
                     r * 16 : r * 16 + 16, b * 128 : (b + 1) * 128
                 ]
 
@@ -263,17 +260,17 @@
         u9, u8 = pair >> 1, pair & 1
         for low in range(32):
             member = (low >> 3) * 32 + u8 * 16 + ((low >> 1) & 3) * 4 + u9 * 2 + (low & 1)
-            block = moved_ref[SLOT3[member]]
+            block = moved_ref[member]
             for u7 in range(2):
                 at = ((pair * 2 + u7) * 32 + low) * 16
                 held_ref[at : at + 16, :] = block[u7 * 16 : u7 * 16 + 16].astype(jnp.float32)
         for u7 in range(2):
             for top in range(4):
                 parts = [
-                    held_ref[pl.ds((pair * 2 + u7) * 512 + top * 4 + j, 32, stride=16), :]
+                    held_ref[pl.ds((pair * 2 + u7) * 512 + top * 4 + j, 32, stride=16), :].astype(jnp.bfloat16)
                     for j in range(4)
                 ]
-                tile = jnp.concatenate(swap_groups(parts), axis=0).astype(jnp.bfloat16)
+                tile = jnp.concatenate(swap_groups(parts), axis=0)
                 out_ref[pair, top * 128 : (top + 1) * 128, u7 * 128 : (u7 + 1) * 128] = product(
                     eye, tile, NT
                 ).astype(jnp.bfloat16)

time: 122 us -> 120 us (0.984)
    all_to_all x3, blocking collectives: 113 us -> 112 us  [exchange(): return lax.all_to_all(value, axes, split_axis=0, concat_axis=0, tiled=True)]
where the time goes in v7:
time: 120 us
  blocking collectives  112 us (93%)
  Pallas kernels  7.82 us (7%)
    all_to_all x3, blocking collectives, exchange(): return lax.all_to_all(value, axes, split_axis=0, concat_axis=0, tiled=True)  112 us
    pallas_call x1, Pallas kernels, step_one(): pl.pallas_call(first_kernel, in_specs=[smem, smem, hbm, hbm], out_specs=[...  3.56 us

profile of v7, /device:TPU:1, one launch (start us, length us, event | category | flops | bytes accessed | tf_op | source)
XLA Modules:
  0.0 120.0 jit_solution(10950267213916429671)
XLA Ops:
  0.0 3.6 %first.1 = (bf16[128,32,128]{2,1,0:T(8,128)(2,1)S(1)}, bf16[512,512]{1,0:T(8,128)(2,1)S(1)}, f32[128,128]{1,0:T(8,128)S(1)}, f32[8,4,8,128]{3,2,1,0:T(8,128)S(1)}) custom-call(s32[14]{0:T(128)} %seed_ref.1, s32[1]{0:T(128)} %bitcast.dev_ref, bf16[512,1024]{1,0:T(8,128)(2,1)} %x_hbm.1, bf16[4,512,512]{2,1,0:T(8,128)(2,1)} %high_ref.1), custom_call_target="tpu_custom_call" | custom-call | flops 1073741824 | bytes 2621440 | tf_op jit(solution)/shard_map/first/pallas_call | solution.py:125
  3.6 55.8 %all_to_all.15.moved_ref = bf16[128,32,128]{2,1,0:T(8,128)(2,1)S(1)} all-to-all(bf16[128,32,128]{2,1,0:T(8,128)(2,1)S(1)} %get-tuple-element.9), channel_id=1, replica_groups=mesh['zh'=2,'core'=2,'x'=4,'z1'=2,'z0'=2,'yh'=4,'y0'=2] {'x','yh','zh','..., dimensions={0} | all-to-all | bytes 2097152 | tf_op jit(solution)/shard_map/all_to_all | solution.py:23
  59.3 0.0 copy-start
  59.3 0.7 second.1
  60.1 15.6 %all_to_all.16 = bf16[16,256,128]{2,1,0:T(8,128)(2,1)S(1)} all-to-all(bf16[16,256,128]{2,1,0:T(8,128)(2,1)S(1)} %bitcast.3), channel_id=1, replica_groups=mesh['zh'=2,'core'=2,'x'=4,'z1'=2,'z0'=2,'yh'=4,'y0'=2] {'x','z0','y0'}, dimensions={0} | all-to-all | bytes 2097152 | tf_op jit(solution)/shard_map/all_to_all | solution.py:23
  75.7 0.0 copy-done
  75.7 1.6 %third.1 = bf16[128,32,128]{2,1,0:T(8,128)(2,1)S(1)} custom-call(bf16[4,4,256,128]{3,2,1,0:T(8,128)(2,1)S(1)} %bitcast.4, bf16[4,512,512]{2,1,0:T(8,128)(2,1)S(1)} %copy-done, bf16[4,512,512]{2,1,0:T(8,128)(2,1)S(1)} %copy-done), custom_call_target="tpu_custom_call" | custom-call | flops 1073741824 | bytes 3145728 | tf_op jit(solution)/shard_map/third/pallas_call | solution.py:234
  77.3 40.8 %all_to_all.17.moved_ref = bf16[128,32,128]{2,1,0:T(8,128)(2,1)S(1)} all-to-all(bf16[128,32,128]{2,1,0:T(8,128)(2,1)S(1)} %third.1), channel_id=1, replica_groups=mesh['zh'=2,'core'=2,'x'=4,'z1'=2,'z0'=2,'yh'=4,'y0'=2] {'yh','y0','zh',..., dimensions={0} | all-to-all | bytes 2097152 | tf_op jit(solution)/shard_map/all_to_all | solution.py:23
  118.1 1.9 %last.1 = bf16[512,1024]{1,0:T(8,128)(2,1)} custom-call(bf16[128,32,128]{2,1,0:T(8,128)(2,1)S(1)} %all_to_all.17.moved_ref), custom_call_target="tpu_custom_call" | custom-call | tf_op jit(solution)/shard_map/last/pallas_call | solution.py:287
Async XLA Ops:
  59.3 16.3 %copy-start = (bf16[4,512,512]{2,1,0:T(8,128)(2,1)S(1)}, bf16[4,512,512]{2,1,0:T(8,128)(2,1)}, u32[]{:S(2)}) copy-start(bf16[4,512,512]{2,1,0:T(8,128)(2,1)} %high_ref.1) | copy-start | bytes 6291460
